TPU v7x, 32 devices: a whole 2x2x4 slice. The times are simulated.
32 devices in a mesh: ctx: 8 (over z, x), inner: 4 (over y, core).
Axes of the slice: x: 2, y: 2, z: 4, core: 2. Of those that a mesh axis runs over, the one named last changes fastest.
Arguments:
- queries: bfloat16 [4096, 512], P(('ctx', 'inner')), may hold values from -8 to 8
- keys: bfloat16 [4096, 512], P(('ctx', 'inner')), may hold values from -6 to 6
- values: bfloat16 [4096, 512], P(('ctx', 'inner')), may hold values from -6 to 6
- w_proj: bfloat16 [8, 64, 256], replicated, may hold values from -1.5 to 1.5
- ln_gain: float32 [2, 64], replicated, may hold values from 0.1 to 1.9
- ln_bias: float32 [2, 64], replicated, may hold values from -3 to 3
- cotangent: bfloat16 [4096, 512], P(('ctx', 'inner')), may hold values from -6 to 6
Outputs:
- attended: bfloat16 [4096, 512], P(('ctx', 'inner'))
- grad_queries: bfloat16 [4096, 512], P(('ctx', 'inner'))
- grad_keys: bfloat16 [4096, 512], P(('ctx', 'inner'))
- grad_values: bfloat16 [4096, 512], P(('ctx', 'inner'))
- grad_proj: float32 [8, 8, 64, 256], P('ctx', None, None, 'inner')
- grad_norm: float32 [4, 64], replicated
All inputs are finite; a program needn't handle non-finite values.
Results may differ from a plain program's by a relative error of at most 0.012.
Values may be sent and summed in bfloat16 or wider, within the bound.
No kernel may reach another device: no remote copies, remote signals or barrier semaphores. Data moves between devices by JAX's collectives and lax.ppermute only.
A program may use at most 64 MiB of HBM per device.

v0:
```python
import math

import jax
import jax.numpy as jnp
from jax import lax
from jax.sharding import PartitionSpec as P

WIN = 128


def with_halo(cells, sides, width):
    for axis, dim in sides:
        count = lax.axis_size(axis)
        ends = count - 1
        head = lax.slice_in_dim(cells, 0, width, axis=dim)
        tail = lax.slice_in_dim(cells, cells.shape[dim] - width, cells.shape[dim], axis=dim)
        cells = jnp.concatenate(
            [
                lax.ppermute(tail, axis, [(i, (i + 1) % count) for i in range(ends)]),
                cells,
                lax.ppermute(head, axis, [((i + 1) % count, i) for i in range(ends)]),
            ],
            axis=dim,
        )
    return cells


def from_behind(block, axis, distance):
    devices = range(lax.axis_size(axis))
    route = [(i - distance, i) for i in devices if i - distance in devices]
    return lax.ppermute(block, axis, route)


def normalise(landmark, gain_row, bias_row):
    average = jnp.mean(landmark, axis=-1, keepdims=True)
    centred = landmark - average
    variance = jnp.mean(centred * centred, axis=-1, keepdims=True)
    inverse = 1.0 / jnp.sqrt(variance + 1e-05)
    normed = centred * inverse
    return (normed, inverse, normed * gain_row + bias_row)


def norm_backward(grad_out, normed, inverse, gain_row):
    grad_normed = grad_out * gain_row
    first_mean = jnp.mean(grad_normed, axis=-1, keepdims=True)
    second_mean = jnp.mean(grad_normed * normed, axis=-1, keepdims=True)
    grad_in = inverse * (grad_normed - first_mean - normed * second_mean)
    return (grad_in, jnp.sum(grad_out * normed, axis=(0, 1)), jnp.sum(grad_out, axis=(0, 1)))


def three_windows(padded, segments, window):
    span = segments * window
    leading = padded.shape[0]
    columns = padded.shape[-1]
    pieces = [
        padded[:, start : start + span].reshape(leading, segments, window, columns)
        for start in (0, window, 2 * window)
    ]
    return jnp.concatenate(pieces, axis=2)


def place_rows(parts, segments, window):
    leading = parts.shape[0]
    columns = parts.shape[-1]
    span = segments * window
    accumulated = jnp.zeros((leading, span + 2 * window, columns), jnp.float32)
    for slot in range(3):
        piece = parts[:, :, slot * window : (slot + 1) * window].reshape(leading, span, columns)
        accumulated = accumulated + jnp.pad(
            piece, ((0, 0), (slot * window, (2 - slot) * window), (0, 0))
        )
    return accumulated


def per_device(queries, keys, values, w_proj, ln_gain, ln_bias, cotangent):
    tokens_dev, features = queries.shape
    heads, head_dim, landmarks = w_proj.shape
    window = WIN
    segments = tokens_dev // window
    edge = 3 * window
    score_scale = 1.0 / math.sqrt(head_dim)
    devices = lax.axis_size("ctx") * lax.axis_size("inner")
    position = lax.axis_index("ctx") * lax.axis_size("inner") + lax.axis_index("inner")
    kv_pad = with_halo(jnp.stack([keys, values]), ((("ctx", "inner"), 1),), window)
    kv_windows = three_windows(kv_pad, segments, window).reshape(2, segments, edge, heads, head_dim)
    key_window = kv_windows[0]
    value_window = kv_windows[1]
    neighbour = (
        position * segments
        + jnp.arange(segments)[:, None]
        - 1
        + jnp.arange(edge)[None, :] // window
    )
    usable = (neighbour >= 0) & (neighbour < devices * segments)
    key_heads = keys.reshape(tokens_dev, heads, head_dim)
    value_heads = values.reshape(tokens_dev, heads, head_dim)
    logits = jnp.einsum("thd,hdr->htr", key_heads, w_proj, preferred_element_type=jnp.float32)
    column_peak = lax.pmax(jnp.max(logits, axis=1), ("ctx", "inner"))
    exponent = jnp.exp(logits - column_peak[:, None, :])
    narrowed = exponent.astype(jnp.bfloat16)
    key_sum = jnp.einsum("htr,thd->hrd", narrowed, key_heads, preferred_element_type=jnp.float32)
    value_sum = jnp.einsum(
        "htr,thd->hrd", narrowed, value_heads, preferred_element_type=jnp.float32
    )
    column_total, key_sum, value_sum = lax.psum(
        (jnp.sum(exponent, axis=1), key_sum, value_sum), ("ctx", "inner")
    )
    mean_keys = key_sum / column_total[..., None]
    mean_values = value_sum / column_total[..., None]
    normed_keys, inverse_keys, land_keys = normalise(mean_keys, ln_gain[0], ln_bias[0])
    normed_values, inverse_values, land_values = normalise(mean_values, ln_gain[1], ln_bias[1])
    land_key_b = land_keys.astype(jnp.bfloat16)
    land_value_b = land_values.astype(jnp.bfloat16)
    query_blocks = queries.reshape(segments, window, heads, head_dim)
    grad_blocks = cotangent.reshape(segments, window, heads, head_dim)
    window_scores = (
        jnp.einsum("sqhd,skhd->shqk", query_blocks, key_window, preferred_element_type=jnp.float32)
        * score_scale
    )
    window_scores = jnp.where(usable[:, None, None, :], window_scores, -1e30)
    land_scores = (
        jnp.einsum("sqhd,hrd->shqr", query_blocks, land_key_b, preferred_element_type=jnp.float32)
        * score_scale
    )
    scores = jnp.concatenate([window_scores, land_scores], axis=-1)
    row_peak = jnp.max(scores, axis=-1)
    log_total = row_peak + jnp.log(jnp.sum(jnp.exp(scores - row_peak[..., None]), axis=-1))
    probs = jnp.exp(scores - log_total[..., None])
    probs_b = probs.astype(jnp.bfloat16)
    output = jnp.einsum(
        "shqk,skhd->sqhd", probs_b[..., :edge], value_window, preferred_element_type=jnp.float32
    )
    output = output + jnp.einsum(
        "shqr,hrd->sqhd", probs_b[..., edge:], land_value_b, preferred_element_type=jnp.float32
    )
    attended = output.astype(jnp.bfloat16).reshape(tokens_dev, features)
    delta = jnp.sum(grad_blocks.astype(jnp.float32) * output, axis=-1).transpose(0, 2, 1)
    grad_window = jnp.einsum(
        "sqhd,skhd->shqk", grad_blocks, value_window, preferred_element_type=jnp.float32
    )
    grad_land = jnp.einsum(
        "sqhd,hrd->shqr", grad_blocks, land_value_b, preferred_element_type=jnp.float32
    )
    grad_probs = jnp.concatenate([grad_window, grad_land], axis=-1)
    grad_scores = (probs * (grad_probs - delta[..., None])).astype(jnp.bfloat16)
    grad_query = jnp.einsum(
        "shqk,skhd->sqhd", grad_scores[..., :edge], key_window, preferred_element_type=jnp.float32
    )
    grad_query = grad_query + jnp.einsum(
        "shqr,hrd->sqhd", grad_scores[..., edge:], land_key_b, preferred_element_type=jnp.float32
    )
    grad_queries = (grad_query * score_scale).astype(jnp.bfloat16).reshape(tokens_dev, features)
    land_key_grad = (
        jnp.einsum(
            "shqr,sqhd->hrd",
            grad_scores[..., edge:],
            query_blocks,
            preferred_element_type=jnp.float32,
        )
        * score_scale
    )
    land_value_grad = jnp.einsum(
        "shqr,sqhd->hrd", probs_b[..., edge:], grad_blocks, preferred_element_type=jnp.float32
    )
    land_key_grad, land_value_grad = lax.psum((land_key_grad, land_value_grad), ("ctx", "inner"))
    part_keys = (
        jnp.einsum(
            "shqk,sqhd->skhd",
            grad_scores[..., :edge],
            query_blocks,
            preferred_element_type=jnp.float32,
        )
        * score_scale
    )
    part_values = jnp.einsum(
        "shqk,sqhd->skhd", probs_b[..., :edge], grad_blocks, preferred_element_type=jnp.float32
    )
    parts = jnp.stack([part_keys, part_values]).reshape(2, segments, edge, features)
    spread_rows = place_rows(parts, segments, window)
    from_right = from_behind(spread_rows[:, :window], ("ctx", "inner"), -1)
    from_left = from_behind(spread_rows[:, tokens_dev + window :], ("ctx", "inner"), 1)
    window_grads = spread_rows[:, window : window + tokens_dev]
    window_grads = window_grads + from_left
    window_grads = window_grads + from_right
    grad_mean_keys, gain_key_grad, bias_key_grad = norm_backward(
        land_key_grad, normed_keys, inverse_keys, ln_gain[0]
    )
    grad_mean_values, gain_value_grad, bias_value_grad = norm_backward(
        land_value_grad, normed_values, inverse_values, ln_gain[1]
    )
    grad_norm = jnp.stack([gain_key_grad, bias_key_grad, gain_value_grad, bias_value_grad])
    grad_key_b = grad_mean_keys.astype(jnp.bfloat16)
    grad_value_b = grad_mean_values.astype(jnp.bfloat16)
    proj_grad = jnp.einsum(
        "thd,hrd->htr", key_heads, grad_key_b, preferred_element_type=jnp.float32
    )
    proj_grad = proj_grad + jnp.einsum(
        "thd,hrd->htr", value_heads, grad_value_b, preferred_element_type=jnp.float32
    )
    weights = narrowed.astype(jnp.float32) / column_total[:, None, :]
    column_sum = jnp.sum(grad_key_b.astype(jnp.float32) * mean_keys, axis=-1) + jnp.sum(
        grad_value_b.astype(jnp.float32) * mean_values, axis=-1
    )
    grad_logit = (weights * (proj_grad - column_sum[:, None, :])).astype(jnp.bfloat16)
    scaled_keys = (grad_mean_keys / column_total[..., None]).astype(jnp.bfloat16)
    scaled_values = (grad_mean_values / column_total[..., None]).astype(jnp.bfloat16)
    land_keys_grad = jnp.einsum(
        "htr,hrd->thd", narrowed, scaled_keys, preferred_element_type=jnp.float32
    )
    land_keys_grad = land_keys_grad + jnp.einsum(
        "htr,hdr->thd", grad_logit, w_proj, preferred_element_type=jnp.float32
    )
    land_values_grad = jnp.einsum(
        "htr,hrd->thd", narrowed, scaled_values, preferred_element_type=jnp.float32
    )
    grad_keys = (window_grads[0] + land_keys_grad.reshape(tokens_dev, features)).astype(
        jnp.bfloat16
    )
    grad_values = (window_grads[1] + land_values_grad.reshape(tokens_dev, features)).astype(
        jnp.bfloat16
    )
    weight_term = jnp.einsum(
        "thd,htr->hdr", key_heads, grad_logit, preferred_element_type=jnp.float32
    )
    grad_proj = lax.psum_scatter(weight_term[None], "inner", scatter_dimension=3, tiled=True)
    return (attended, grad_queries, grad_keys, grad_values, grad_proj, grad_norm)


def solution(mesh):
    return jax.shard_map(
        per_device,
        mesh=mesh,
        in_specs=(
            P(("ctx", "inner"), None),
            P(("ctx", "inner"), None),
            P(("ctx", "inner"), None),
            P(),
            P(),
            P(),
            P(("ctx", "inner"), None),
        ),
        out_specs=(
            P(("ctx", "inner"), None),
            P(("ctx", "inner"), None),
            P(("ctx", "inner"), None),
            P(("ctx", "inner"), None),
            P("ctx", None, None, "inner"),
            P(),
        ),
        check_vma=False,
    )
```

profile of v0, /device:TPU:0, one launch (start us, length us, event | category | flops | bytes accessed | tf_op | source)
XLA Modules:
  0.0 388.1 jit_solution(10665908590580263117)
XLA Ops:
  8.3 1.3 collective-permute-start.1
  9.6 3.0 collective-permute-start
  15.1 42.8 %pmax.7 = f32[8,256]{1,0:T(8,128)S(1)} all-reduce(f32[8,256]{1,0:T(8,128)S(1)} %get-tuple-element.64), channel_id=1, replica_groups=mesh['ctx'=8,'inner'=4] {'ctx','inner'}, use_global_device_ids=true, to_apply=%region_1.2 | all-reduce | flops 2048 | bytes 16384 | tf_op jit(solution)/shard_map/pmax | solution.py:98
  61.4 40.5 %psum.36 = f32[8,256]{1,0:T(8,128)S(1)} all-reduce(f32[8,256]{1,0:T(8,128)S(1)} %get-tuple-element.50), channel_id=1, replica_groups=mesh['ctx'=8,'inner'=4] {'ctx','inner'}, use_global_device_ids=true, to_apply=%region_4.5 | all-reduce | flops 2048 | bytes 16384 | tf_op jit(solution)/shard_map/psum | solution.py:105
  103.0 1.6 convolution_bitcast_fusion
  105.2 87.9 %all-reduce.10.cloned.1.call-done = (f32[8,256,64]{1,2,0:T(8,128)}, f32[8,256,64]{1,2,0:T(8,128)}) async-done(((f32[8,256,64]{1,2,0:T(8,128)}, f32[8,256,64]{1,2,0:T(8,128)}), (f32[8,256,64]{1,2,0:T(8,128)}, f32[8,256,64]{1,2,0:T(8,128)})) %all-reduce.10.cloned.1.call-update) | async-done | bytes 1048592 | tf_op jit(solution)/shard_map/psum | solution.py:105
  193.1 1.4 fusion.37
  194.5 1.4 multiply_reduce_fusion.6
  202.5 1.4 convolution_multiply_fusion.1
  205.0 1.4 fusion.15
  206.4 1.4 fusion.12
  211.4 2.1 collective-permute-start.2
  213.5 1.5 collective-permute-start.3
  215.0 125.2 %all-reduce.8.cloned.1.call-done = (f32[8,256,64]{1,2,0:T(8,128)}, f32[8,256,64]{1,2,0:T(8,128)}) async-done(((f32[8,256,64]{1,2,0:T(8,128)}, f32[8,256,64]{1,2,0:T(8,128)}), (f32[8,256,64]{1,2,0:T(8,128)}, f32[8,256,64]{1,2,0:T(8,128)})) %all-reduce.8.cloned.1.call-update) | async-done | bytes 1048592 | tf_op jit(solution)/shard_map/psum | solution.py:165
  340.2 1.3 multiply_reduce_fusion.8
  341.6 2.4 multiply_reduce_fusion.9
  344.1 1.2 multiply_reduce_fusion.1
  345.3 1.4 fusion.30
  347.8 1.8 copy.89
  350.3 1.9 fusion.7
  354.1 2.4 copy.102
  356.5 2.3 reshape.429
  361.2 1.3 fusion.20
  363.4 16.3 %reduce-scatter.4.cloned.1.call-done = f32[64,512]{1,0:T(8,128)} async-done(((f32[256,512]{1,0:T(8,128)}), f32[64,512]{1,0:T(8,128)}) %reduce-scatter.4.cloned.1.call-update) | async-done | bytes 131088
  (193 shorter events, 28.2 us)
Async XLA Ops:
  7.2 7.6 %copy-start = (bf16[8,64,256]{2,1,0:T(8,128)(2,1)S(1)}, bf16[8,64,256]{2,1,0:T(8,128)(2,1)}, u32[]{:S(2)}) copy-start(bf16[8,64,256]{2,1,0:T(8,128)(2,1)} %param.10) | copy-start | bytes 786436
  7.2 185.9 %all-reduce.10.cloned.1.call-start = ((), (), s32[]{:S(2)}) async-start(), calls=%async_computation.3 | async-start | bytes 2097152 | tf_op jit(solution)/shard_map/psum | solution.py:105
  8.3 94.2 %collective-permute-start.1 = (bf16[2,128,512]{2,1,0:T(8,128)(2,1)S(1)}, bf16[2,128,512]{2,1,0:T(8,128)(2,1)S(1)}, u32[]{:S(2)}, u32[]{:S(2)}) collective-permute-start(bf16[2,128,512]{2,1,0:T(8,128)(2,1)S(1)} %get-tuple-element.59), channel_id=1, source_target_pairs={{1,0},{2,1},{3,2},{4,3},{5,4},{6,5},{7,6},{8,7},{9,8},{10,9},{11,1... | collective-permute-start | bytes 786440 | tf_op jit(solution)/shard_map/ppermute | solution.py:21
  9.6 92.9 %collective-permute-start = (bf16[2,128,512]{2,1,0:T(8,128)(2,1)S(1)}, bf16[2,128,512]{2,1,0:T(8,128)(2,1)S(1)}, u32[]{:S(2)}, u32[]{:S(2)}) collective-permute-start(bf16[2,128,512]{2,1,0:T(8,128)(2,1)S(1)} %get-tuple-element.59), channel_id=1, source_target_pairs={{0,1},{1,2},{2,3},{3,4},{4,5},{5,6},{6,7},{7,8},{8,9},{9,10},{10,1... | collective-permute-start | bytes 786440 | tf_op jit(solution)/shard_map/ppermute | solution.py:19
  13.7 44.5 %copy-start.18 = (bf16[128,512]{0,1:T(8,128)(2,1)}, bf16[128,512]{0,1:T(8,128)(2,1)S(1)}, u32[]{:S(2)}) copy-start(bf16[128,512]{0,1:T(8,128)(2,1)S(1)} %copy.72) | copy-start | bytes 393220
  14.7 87.8 %copy-start.27 = (bf16[128,512]{0,1:T(8,128)(2,1)}, bf16[128,512]{0,1:T(8,128)(2,1)S(1)}, u32[]{:S(2)}) copy-start(bf16[128,512]{0,1:T(8,128)(2,1)S(1)} %copy.74) | copy-start | bytes 393220
  59.2 42.7 %copy-start.60 = (f32[2,64]{1,0:T(2,128)S(1)}, f32[2,64]{1,0:T(2,128)}, u32[]{:S(2)}) copy-start(f32[2,64]{1,0:T(2,128)} %param.12) | copy-start | bytes 1540
  59.2 42.7 %copy-start.61 = (f32[2,64]{1,0:T(2,128)S(1)}, f32[2,64]{1,0:T(2,128)}, u32[]{:S(2)}) copy-start(f32[2,64]{1,0:T(2,128)} %param.11) | copy-start | bytes 1540
  60.3 279.9 %all-reduce.8.cloned.1.call-start = ((), (), s32[]{:S(2)}) async-start(), calls=%async_computation.2 | async-start | bytes 2097152 | tf_op jit(solution)/shard_map/psum | solution.py:165
  60.5 42.5 %copy-start.20 = (bf16[128,512]{0,1:T(8,128)(2,1)}, bf16[128,512]{0,1:T(8,128)(2,1)S(1)}, u32[]{:S(2)}) copy-start(bf16[128,512]{0,1:T(8,128)(2,1)S(1)} %copy.76) | copy-start | bytes 393220
  61.4 134.5 %copy-start.23 = (bf16[128,512]{0,1:T(8,128)(2,1)}, bf16[128,512]{0,1:T(8,128)(2,1)S(1)}, u32[]{:S(2)}) copy-start(bf16[128,512]{0,1:T(8,128)(2,1)S(1)} %copy.71) | copy-start | bytes 393220
  102.4 93.5 %copy-start.48 = (f32[64]{0:T(128)}, f32[64]{0:T(128)S(1)}, u32[]{:S(2)}) copy-start(f32[64]{0:T(128)S(1)} %get-tuple-element.73) | copy-start | bytes 772
  102.4 93.5 %copy-start.62 = (f32[64]{0:T(128)}, f32[64]{0:T(128)S(1)}, u32[]{:S(2)}) copy-start(f32[64]{0:T(128)S(1)} %get-tuple-element.63) | copy-start | bytes 772
  210.0 169.7 %reduce-scatter.4.cloned.1.call-start = ((), (), s32[]{:S(2)}) async-start(), calls=%async_computation.1 | async-start | bytes 655360
  210.3 129.9 %copy-start.5 = (f32[8,256,64]{1,2,0:T(8,128)S(1)}, f32[8,256,64]{1,2,0:T(8,128)}, u32[]{:S(2)}) copy-start(f32[8,256,64]{1,2,0:T(8,128)} %get-tuple-element.43) | copy-start | bytes 1572868
  210.3 129.9 %copy-start.30 = (f32[8,256]{1,0:T(8,128)S(1)}, f32[8,256]{1,0:T(8,128)}, u32[]{:S(2)}) copy-start(f32[8,256]{1,0:T(8,128)} %copy-done.29) | copy-start | bytes 24580
  210.3 129.9 %copy-start.40 = (f32[8,256]{1,0:T(8,128)S(1)}, f32[8,256]{1,0:T(8,128)}, u32[]{:S(2)}) copy-start(f32[8,256]{1,0:T(8,128)} %copy-done.39) | copy-start | bytes 24580
  210.3 129.9 %copy-start.54 = (f32[64]{0:T(128)S(1)}, f32[64]{0:T(128)}, u32[]{:S(2)}) copy-start(f32[64]{0:T(128)} %get-tuple-element.74) | copy-start | bytes 772
  210.3 131.2 %copy-start.36 = (f32[8,256]{1,0:T(8,128)S(1)}, f32[8,256]{1,0:T(8,128)}, u32[]{:S(2)}) copy-start(f32[8,256]{1,0:T(8,128)} %copy-done.34) | copy-start | bytes 24580
  210.3 131.2 %copy-start.50 = (f32[64]{0:T(128)S(1)}, f32[64]{0:T(128)}, u32[]{:S(2)}) copy-start(f32[64]{0:T(128)} %copy-done.48) | copy-start | bytes 772
  211.4 149.8 %collective-permute-start.2 = (f32[2,128,512]{2,1,0:T(8,128)}, f32[2,128,512]{2,1,0:T(8,128)}, u32[]{:S(2)}, u32[]{:S(2)}) collective-permute-start(f32[2,128,512]{2,1,0:T(8,128)} %get-tuple-element.45), channel_id=1, source_target_pairs={{0,1},{1,2},{2,3},{3,4},{4,5},{5,6},{6,7},{7,8},{8,9},{9,10},{10,1... | collective-permute-start | bytes 1572872 | tf_op jit(solution)/shard_map/ppermute | solution.py:31
  213.5 147.7 %collective-permute-start.3 = (f32[2,128,512]{2,1,0:T(8,128)}, f32[2,128,512]{2,1,0:T(8,128)}, u32[]{:S(2)}, u32[]{:S(2)}) collective-permute-start(f32[2,128,512]{2,1,0:T(8,128)} %get-tuple-element.46), channel_id=1, source_target_pairs={{1,0},{2,1},{3,2},{4,3},{5,4},{6,5},{7,6},{8,7},{9,8},{10,9},{11,1... | collective-permute-start | bytes 1572872 | tf_op jit(solution)/shard_map/ppermute | solution.py:31
  341.5 5.2 %copy-start.46 = (f32[8,256]{1,0:T(8,128)}, f32[8,256]{1,0:T(8,128)S(1)}, u32[]{:S(2)}) copy-start(f32[8,256]{1,0:T(8,128)S(1)} %broadcast_multiply_fusion.1) | copy-start | bytes 24580
  341.5 5.2 %copy-start.47 = (f32[8,256]{1,0:T(8,128)}, f32[8,256]{1,0:T(8,128)S(1)}, u32[]{:S(2)}) copy-start(f32[8,256]{1,0:T(8,128)S(1)} %broadcast_multiply_fusion) | copy-start | bytes 24580
  (48 other events, 108.0 us)
Sparse Core Ops, SparseCore 0:
  60.4 132.6 all-reduce.9
  210.1 130.0 all-reduce.7
  359.0 20.6 reduce-scatter.3
where the time goes:
time: 389 us; the launch traced here: 388 us
  waiting for transfers between devices  230 us (59%)
  blocking collectives  83.3 us (21%)
  local copies, waits for them, and re-layouts  19.4 us (5%)
  matrix products  19.3 us (5%)
  between operations  14.7 us (4%)
  other arithmetic  13.9 us (4%)
  starting transfers between devices  8.01 us (2%)
    psum x1, waiting for transfers between devices, per_device(): lax.psum((land_key_grad, land_value_grad), ('ctx', 'inner'))  125 us
    psum x1, waiting for transfers between devices, per_device(): lax.psum((jnp.sum(exponent, axis=1), key_sum, value_sum), ('ctx', 'inner'))  87.9 us
    pmax x1, blocking collectives, per_device(): column_peak = lax.pmax(jnp.max(logits, axis=1), ('ctx', 'inner'))  42.8 us
    psum x1, blocking collectives, per_device(): lax.psum((jnp.sum(exponent, axis=1), key_sum, value_sum), ('ctx', 'inner'))  40.5 us
    unnamed x4, waiting for transfers between devices  16.4 us
    unnamed x140, local copies, waits for them, and re-layouts  14.1 us
  transfers between devices with their start and end apart: 7, of which 3 were waited for; matrix products, arithmetic and copies ran while one was open for 8% of the time, Pallas kernels for 0%

commit v1 on v0

v1 whole, which is shorter than its diff:
```python
import functools
import math

import jax
import jax.numpy as jnp
import numpy as np
from jax import lax
from jax.experimental import pallas as pl
from jax.experimental.pallas import tpu as pltpu
from jax.sharding import Mesh
from jax.sharding import PartitionSpec as P

WIN = 128
EXTRA = 16
EPS = 1e-05
NEG = -1e30
BF = jnp.bfloat16
F32 = jnp.float32

NN = (((1,), (0,)), ((), ()))
NT = (((1,), (1,)), ((), ()))
SEQ = ("seq", "half")
HEAD = ("sub", "part")


def dot(a, b, dims=NN):
    return lax.dot_general(a, b, dims, preferred_element_type=F32)


def lanes(shape):
    return lax.broadcasted_iota(jnp.int32, shape, 1)


def rows(shape):
    return lax.broadcasted_iota(jnp.int32, shape, 0)


def pack_kernel(q_ref, k_ref, v_ref, g_ref, o_ref):
    heads, _, width = o_ref.shape
    dh = width // 4
    for h in range(heads):
        cols = slice(h * dh, (h + 1) * dh)
        for slot, ref in enumerate((k_ref, v_ref, q_ref, g_ref)):
            o_ref[h, :, slot * dh : (slot + 1) * dh] = ref[:, cols]


def split_rows(total_rows, width, pieces):
    r = rows((total_rows, width))
    out = jnp.zeros((total_rows, width), F32)
    for index, piece in enumerate(pieces):
        out = jnp.where(r == index, piece, out)
    return out.astype(BF)


def bf_pieces(x, count):
    out = []
    for _ in range(count):
        piece = x.astype(BF).astype(F32)
        out.append(piece)
        x = x - piece
    return out


def widen_proj(w):
    return jnp.concatenate([w, jnp.zeros_like(w)], axis=0)


def local_sums_kernel(h_ref, x_ref, w_ref, mid_ref, *out_refs):
    del h_ref
    expo_ref = out_refs[-1]
    pair = x_ref.shape[1] // 2
    kv = x_ref[:, :pair]
    logits = dot(kv, widen_proj(w_ref[0]))
    peak = jnp.max(logits, axis=0, keepdims=True)
    expo = jnp.exp(logits - peak)
    total = jnp.sum(expo, axis=0, keepdims=True)
    expo_b = expo.astype(BF)
    expo_ref[...] = expo_b
    sums = dot(kv.T, expo_b).astype(BF)
    marks = sums.shape[1]
    tail = split_rows(EXTRA, marks, bf_pieces(peak, 3) + bf_pieces(total, 2))
    targets = [(mid_ref, None)]
    if len(out_refs) == 3:
        count = x_ref.shape[0]
        targets += [(out_refs[0], kv[count - WIN :]), (out_refs[1], kv[:WIN])]
    for ref, halo in targets:
        ref[:pair, :marks] = sums
        ref[pair:, :marks] = tail
        if halo is not None:
            ref[:pair, marks:] = halo
            ref[pair:, marks:] = jnp.zeros((EXTRA, pair), BF)


def collect(own_ref, recv_refs, stack_ref, index, marks):
    count = len(recv_refs) + 1
    stack_ref[index] = own_ref[...]
    for shift, ref in enumerate(recv_refs, start=1):
        stack_ref[lax.rem(index + (count - shift), count)] = ref[:, :marks]


def attention_kernel(*refs, ring, scale):
    if ring > 0:
        z_ref, x_ref, own_ref, *recv = refs[:3 + ring]
        gain_ref, bias_ref = refs[3 + ring : 5 + ring]
        rest = refs[5 + ring :]
    else:
        z_ref, x_ref, stack_ref, prev_ref, next_ref, gain_ref, bias_ref = refs[:7]
        rest = refs[7:]
    count, width = x_ref.shape
    pair = width // 2
    dh = pair // 2
    segments = count // WIN
    if ring > 0:
        od_ref, dkvt_ref, mid_ref, plus_ref, minus_ref, stats_ref, kvp_ref, acc_ref, stack_ref = rest
    else:
        od_ref, dkvt_ref, mid_ref, plus_ref, minus_ref, stats_ref, kvp_ref, acc_ref = rest
    marks = mid_ref.shape[1]
    z = z_ref[0]
    last = z_ref[1] - 1
    if ring > 0:
        collect(own_ref, recv, stack_ref, z, marks)
        prev_halo = recv[0][:pair, marks:]
        next_halo = recv[-1][:pair, marks:]
    else:
        prev_halo = prev_ref[...]
        next_halo = next_ref[...]
    groups = stack_ref.shape[0]
    kvp_ref[:WIN] = prev_halo
    kvp_ref[WIN : WIN + count] = x_ref[:, :pair]
    kvp_ref[WIN + count :] = next_halo

    peaks, totals = [], []
    for j in range(groups):
        tail = stack_ref[j, pair:, :].astype(F32)
        peaks.append(tail[0:1] + tail[1:2] + tail[2:3])
        totals.append(tail[3:4] + tail[4:5])
    peak = functools.reduce(jnp.maximum, peaks)
    total = jnp.zeros_like(peak)
    sums = jnp.zeros((pair, marks), F32)
    for j in range(groups):
        factor = jnp.exp(peaks[j] - peak)
        total = total + factor * totals[j]
        sums = sums + factor * stack_ref[j, :pair, :].astype(F32)
    mean = sums / total
    normed, inverse = [], []
    for half in range(2):
        block = mean[half * dh : (half + 1) * dh]
        centred = block - jnp.mean(block, axis=0, keepdims=True)
        variance = jnp.mean(centred * centred, axis=0, keepdims=True)
        inv = 1.0 / jnp.sqrt(variance + EPS)
        normed.append(centred * inv)
        inverse.append(inv)
    normed = jnp.concatenate(normed, axis=0)
    land_f = normed * gain_ref[...] + bias_ref[...]
    land_t = land_f.astype(BF)
    land = land_f.T.astype(BF)
    stack_own = stack_ref[z, pair:, :].astype(F32)
    own_peak = stack_own[0:1] + stack_own[1:2] + stack_own[2:3]
    factor = jnp.exp(own_peak - peak) / total
    stats_ref[:pair] = normed
    stats_ref[pair : 2 * pair] = mean
    r8 = rows((8, marks))
    stats_ref[2 * pair :] = jnp.where(r8 == 0, inverse[0], jnp.where(r8 == 1, inverse[1], factor))

    acc_ref[...] = jnp.zeros(acc_ref.shape, F32)
    land_grad = jnp.zeros((pair, marks), F32)
    low = lanes((WIN, pair)) < dh
    zero_b = jnp.zeros((WIN, pair), BF)
    for s in range(segments):
        qg = x_ref[s * WIN : (s + 1) * WIN, pair:]
        q0 = jnp.where(low, (qg.astype(F32) * scale).astype(BF), zero_b)
        g0 = jnp.where(low, zero_b, qg)
        a = jnp.concatenate([q0, g0], axis=0)
        kvw = kvp_ref[s * WIN : (s + 3) * WIN]
        sw = dot(a, kvw, NT)
        sl = dot(a, land_t)
        s_w, gp_w = sw[:WIN], sw[WIN:]
        s_l, gp_l = sl[:WIN], sl[WIN:]
        if s == 0:
            s_w = jnp.where((lanes(s_w.shape) < WIN) & (z == 0), NEG, s_w)
        if s == segments - 1:
            s_w = jnp.where((lanes(s_w.shape) >= 2 * WIN) & (z == last), NEG, s_w)
        top = jnp.maximum(
            jnp.max(s_w, axis=1, keepdims=True), jnp.max(s_l, axis=1, keepdims=True)
        )
        e_w = jnp.exp(s_w - top)
        e_l = jnp.exp(s_l - top)
        inv = 1.0 / (
            jnp.sum(e_w, axis=1, keepdims=True) + jnp.sum(e_l, axis=1, keepdims=True)
        )
        p_w = e_w * inv
        p_l = e_l * inv
        pb_w = p_w.astype(BF)
        pb_l = p_l.astype(BF)
        delta = jnp.sum(pb_w.astype(F32) * gp_w, axis=1, keepdims=True) + jnp.sum(
            pb_l.astype(F32) * gp_l, axis=1, keepdims=True
        )
        b_w = jnp.concatenate([(p_w * (gp_w - delta)).astype(BF), pb_w], axis=0)
        b_l = jnp.concatenate([(p_l * (gp_l - delta)).astype(BF), pb_l], axis=0)
        od = dot(b_w, kvw) + dot(b_l, land)
        od_ref[s * WIN : (s + 1) * WIN] = jnp.where(low, od[:WIN] * scale, od[WIN:]).astype(BF)
        at = a.T
        acc_ref[:, s * WIN : (s + 3) * WIN] += dot(at, b_w)
        land_grad = land_grad + dot(at, b_l)
    dkvt_ref[...] = acc_ref[:, WIN : WIN + count]
    land_b = land_grad.astype(BF)
    mid_ref[...] = land_b
    if ring > 0:
        plus_ref[:, :marks] = land_b
        plus_ref[:, marks:] = acc_ref[:, WIN + count :].astype(BF)
        minus_ref[:, :marks] = land_b
        minus_ref[:, marks:] = acc_ref[:, :WIN].astype(BF)
    else:
        plus_ref[...] = acc_ref[:, WIN + count :].astype(BF)
        minus_ref[...] = acc_ref[:, :WIN].astype(BF)


def final_kernel(*refs, ring, sub, parts, tiled):
    if ring > 0:
        z_ref, own_ref, *recv = refs[: 2 + ring]
        rest = refs[2 + ring :]
    else:
        z_ref, stack_ref, prev_ref, next_ref = refs[:4]
        rest = refs[4:]
    x_ref, w_ref, gain_ref, expo_ref, od_ref, dkvt_ref, stats_ref = rest[:7]
    outs = rest[7:]
    send_ref = outs[0]
    count, width = x_ref.shape
    pair = width // 2
    dh = pair // 2
    marks = expo_ref.shape[1]
    z = z_ref[0]
    last = z_ref[1] - 1
    if ring > 0:
        stack_ref = outs[-1]
        collect(own_ref, recv, stack_ref, z, marks)
        from_prev = recv[0][:, marks:]
        from_next = recv[-1][:, marks:]
    else:
        from_prev = prev_ref[...]
        from_next = next_ref[...]
    from_prev = jnp.where(z == 0, 0.0, from_prev.astype(F32))
    from_next = jnp.where(z == last, 0.0, from_next.astype(F32))
    grad = stack_ref[0].astype(F32)
    for j in range(1, stack_ref.shape[0]):
        grad = grad + stack_ref[j].astype(F32)
    normed = stats_ref[:pair]
    mean = stats_ref[pair : 2 * pair]
    factor = stats_ref[2 * pair + 2 : 2 * pair + 3]
    gained = grad * gain_ref[...]
    blocks = []
    for half in range(2):
        part = slice(half * dh, (half + 1) * dh)
        g = gained[part]
        first = jnp.mean(g, axis=0, keepdims=True)
        second = jnp.mean(g * normed[part], axis=0, keepdims=True)
        inv = stats_ref[2 * pair + half : 2 * pair + half + 1]
        blocks.append(inv * (g - first - normed[part] * second))
    grad_mean = jnp.concatenate(blocks, axis=0)
    grad_b = grad_mean.astype(BF)
    column = jnp.sum(grad_b.astype(F32) * mean, axis=0, keepdims=True)
    scaled = (grad_mean * factor).astype(BF)

    gain_sum = jnp.sum(grad * normed, axis=1, keepdims=True)
    bias_sum = jnp.sum(grad, axis=1, keepdims=True)
    lane = lanes((pair, pair))
    square = jnp.where(lane == 0, gain_sum, jnp.where(lane == 1, bias_sum, 0.0)).T
    norm_hi = square[:8].astype(BF)
    norm_lo = (square[:8] - norm_hi.astype(F32)).astype(BF)
    norm_rows = jnp.concatenate(
        [
            jnp.concatenate([norm_hi.astype(F32), norm_lo.astype(F32)], axis=1),
            jnp.zeros((8, width), F32),
        ],
        axis=0,
    ).astype(BF)

    kv = x_ref[:, :pair]
    wide = widen_proj(w_ref[0])
    expo_b = expo_ref[...]
    weights = expo_b.astype(F32) * factor
    grad_logit = (weights * (dot(kv, grad_b) - column)).astype(BF)
    land = dot(expo_b, scaled, NT) + dot(grad_logit, wide, NT)
    window = dkvt_ref[...].T
    dests, out_rows, _ = send_ref.shape
    step = count // dests
    dkv = land + window
    head_fix = from_prev.T
    tail_fix = from_next.T
    for d in range(dests):
        span = slice(d * step, (d + 1) * step)
        block = dkv[span]
        fix_top = head_fix if d == 0 else None
        fix_end = tail_fix if d == dests - 1 else None
        for at in range(0, step, WIN):
            piece = block[at : at + WIN]
            if fix_top is not None and at == 0:
                piece = piece + fix_top
            if fix_end is not None and at + WIN == step:
                piece = piece + fix_end
            send_ref[d, at : at + WIN, :pair] = piece.astype(BF)
        send_ref[d, :step, pair:] = od_ref[span]
        send_ref[d, step : step + 16] = norm_rows
    kvt = kv.T
    group = count // sub
    for sb in range(sub):
        span = slice(sb * group, (sb + 1) * group)
        proj = dot(kvt[:, span], grad_logit[span])[:dh]
        if tiled:
            wide_part = marks // parts
            quarter = dh // 4
            for i in range(parts):
                tile = proj[:, i * wide_part : (i + 1) * wide_part].astype(BF)
                for k in range(4):
                    send_ref[
                        sb * parts + i, step + 16 :, k * dh : (k + 1) * dh
                    ] = tile[k * quarter : (k + 1) * quarter]
        else:
            outs[1][...] = proj


def unpack_kernel(r_ref, att_ref, dq_ref, dk_ref, dv_ref, norm_ref, *proj_refs):
    heads, _, width = r_ref.shape
    dh = width // 4
    pair = 2 * dh
    step = att_ref.shape[0]
    for h in range(heads):
        cols = slice(h * dh, (h + 1) * dh)
        for slot, ref in enumerate((dk_ref, dv_ref, dq_ref, att_ref)):
            ref[:, cols] = r_ref[h, :step, slot * dh : (slot + 1) * dh]
    norm = jnp.zeros((8, pair), F32)
    for h in range(heads):
        block = r_ref[h, step : step + 16, :].astype(F32)[:8]
        norm = norm + (block[:, :pair] + block[:, pair:])
    norm_ref[0:1] = norm[0:1, :dh]
    norm_ref[1:2] = norm[1:2, :dh]
    norm_ref[2:3] = norm[0:1, dh:]
    norm_ref[3:4] = norm[1:2, dh:]
    if proj_refs:
        proj_ref = proj_refs[0]
        quarter = dh // 4
        for h in range(heads):
            for k in range(4):
                proj_ref[0, h, k * quarter : (k + 1) * quarter] = r_ref[
                    h, step + 16 :, k * dh : (k + 1) * dh
                ].astype(F32)


def shape_of(shape, dtype):
    return jax.ShapeDtypeStruct(shape, dtype)


VM = pl.BlockSpec(memory_space=pltpu.VMEM)
SM = pl.BlockSpec(memory_space=pltpu.SMEM)


def call(kernel, out_shape, args, specs, name, scratch=()):
    return pl.pallas_call(
        kernel,
        out_shape=out_shape,
        in_specs=specs,
        out_specs=jax.tree.map(lambda _: VM, out_shape),
        scratch_shapes=scratch,
        name=name,
    )(*args)


def per_device(queries, keys, values, w_proj, ln_gain, ln_bias, cotangent):
    tokens_dev, features = queries.shape
    heads, dh, marks = w_proj.shape
    pair = 2 * dh
    width = 4 * dh
    count = tokens_dev * heads
    scale = 1.0 / math.sqrt(dh)
    seqs = lax.axis_size(SEQ)
    sub = lax.axis_size("sub")
    parts = lax.axis_size("part")
    halves = lax.axis_size("half")
    head = lax.axis_index(HEAD).astype(jnp.int32)
    z = lax.axis_index(SEQ).astype(jnp.int32)
    place = jnp.stack([z, jnp.int32(seqs)])
    ring = seqs - 1 if 3 <= seqs <= 8 else 0
    wide_part = marks // parts
    tiled = halves == 1 and wide_part == dh and dh % 64 == 0

    packed = call(
        pack_kernel,
        shape_of((heads, tokens_dev, width), BF),
        (queries, keys, values, cotangent),
        [VM] * 4,
        "pack",
    )
    x = lax.all_to_all(packed, HEAD, 0, 0, tiled=True).reshape(count, width)
    w_head = lax.dynamic_slice_in_dim(w_proj, head, 1, axis=0)

    rows_out = pair + EXTRA
    out_shape = [shape_of((rows_out, marks), BF)]
    if ring:
        out_shape += [shape_of((rows_out, marks + pair), BF)] * 2
    out_shape.append(shape_of((count, marks), BF))
    mid, *halo_outs, expo = call(
        local_sums_kernel, out_shape, (place, x, w_head), [SM, VM, VM], "local_sums"
    )

    def shifted(block, shift):
        return lax.ppermute(block, SEQ, [(i, (i + shift) % seqs) for i in range(seqs)])

    def forward(block, shift):
        route = [(i, i + shift) for i in range(seqs) if 0 <= i + shift < seqs]
        return lax.ppermute(block, SEQ, route)

    gain = ln_gain.reshape(pair, 1)
    bias = ln_bias.reshape(pair, 1)
    if ring:
        recv = [shifted(halo_outs[0], 1)]
        recv += [shifted(mid, k) for k in range(2, ring)]
        recv += [shifted(halo_outs[1], ring)]
        lands = [mid, *recv]
    else:
        lands = [
            lax.all_gather(mid, SEQ),
            forward(x[count - WIN :, :pair], 1),
            forward(x[:WIN, :pair], -1),
        ]
    halo_wide = marks + pair if ring else pair
    scratch = [pltpu.VMEM((count + 2 * WIN, pair), BF), pltpu.VMEM((pair, count + 2 * WIN), F32)]
    if ring:
        scratch.append(pltpu.VMEM((seqs, rows_out, marks), BF))
    od, dkvt, grad_mid, plus, minus, stats = call(
        functools.partial(attention_kernel, ring=ring, scale=scale),
        [
            shape_of((count, pair), BF),
            shape_of((pair, count), F32),
            shape_of((pair, marks), BF),
            shape_of((pair, halo_wide), BF),
            shape_of((pair, halo_wide), BF),
            shape_of((2 * pair + 8, marks), F32),
        ],
        (place, x, *lands, gain, bias),
        [SM] + [VM] * (len(lands) + 3),
        "attention",
        scratch,
    )
    if ring:
        recv = [shifted(plus, 1)]
        recv += [shifted(grad_mid, k) for k in range(2, ring)]
        recv += [shifted(minus, ring)]
        grads = [grad_mid, *recv]
        scratch = [pltpu.VMEM((seqs, pair, marks), BF)]
    else:
        grads = [lax.all_gather(grad_mid, SEQ), forward(plus, 1), forward(minus, -1)]
        scratch = []
    send_rows = tokens_dev + 16 + (dh // 4 if tiled else 0)
    out_shape = [shape_of((heads, send_rows, width), BF)]
    if not tiled:
        out_shape.append(shape_of((dh, marks), F32))
    send, *proj = call(
        functools.partial(
            final_kernel, ring=ring, sub=sub if tiled else 1, parts=parts, tiled=tiled
        ),
        out_shape,
        (place, *grads, x, w_head, gain, expo, od, dkvt, stats),
        [SM] + [VM] * (len(grads) + 7),
        "landmark_backward",
        scratch,
    )
    back = lax.all_to_all(send, HEAD, 0, 0, tiled=True)
    out_shape = [shape_of((tokens_dev, features), BF)] * 4 + [shape_of((4, dh), F32)]
    if tiled:
        out_shape.append(shape_of((1, heads, dh, wide_part), F32))
    attended, dq, dk, dv, grad_norm, *tiles = call(unpack_kernel, out_shape, (back,), [VM], "unpack")
    if tiled:
        grad_proj = tiles[0]
    else:
        full = lax.all_gather(proj[0], HEAD)
        inner = ("half", "part") if halves > 1 else "part"
        grad_proj = lax.psum_scatter(full, inner, scatter_dimension=2, tiled=True)[None] / parts
    return (attended, dq, dk, dv, grad_proj, grad_norm)


def solution(mesh):
    ctx, inner = mesh.shape["ctx"], mesh.shape["inner"]

    def whole(queries, keys, values, w_proj, ln_gain, ln_bias, cotangent):
        heads = w_proj.shape[0]
        part = min(heads, inner)
        sub = heads // part
        order = np.asarray(mesh.devices).reshape(ctx // sub, sub, inner // part, part)
        split = Mesh(order, ("seq", "sub", "half", "part"))
        every = P(("seq", "sub", "half", "part"), None)
        return jax.shard_map(
            per_device,
            mesh=split,
            in_specs=(every, every, every, P(), P(), P(), every),
            out_specs=(
                every,
                every,
                every,
                every,
                P(("seq", "sub"), None, None, ("half", "part")),
                P(),
            ),
            check_vma=False,
        )(queries, keys, values, w_proj, ln_gain, ln_bias, cotangent)

    return whole
```

time: 389 us -> 73.1 us (0.19)
  waiting for transfers between devices: 230 us -> 19.9 us
  blocking collectives: 83.3 us -> 15 us
  matrix products: 19.3 us -> 0 us
  Pallas kernels: 0 us -> 17.9 us
  local copies, waits for them, and re-layouts: 19.4 us -> 4.95 us
  between operations: 14.7 us -> 0.68 us
  other arithmetic: 13.9 us -> 0.59 us
  starting transfers between devices: 8.01 us -> 13.6 us
    psum x2 -> x0, waiting for transfers between devices: 213 us -> none  [the longest x1 125 us: per_device(): lax.psum((land_key_grad, land_value_grad), ('ctx', 'inner'))]
    pmax x1 -> x0, blocking collectives: 42.8 us -> none  [per_device(): column_peak = lax.pmax(jnp.max(logits, axis=1), ('ctx', 'inner'))]
    psum x1 -> x0, blocking collectives: 40.5 us -> none  [per_device(): lax.psum((jnp.sum(exponent, axis=1), key_sum, value_sum), ('ctx', 'inner'))]
    dot_general x21 -> x0, matrix products: 19.3 us -> none  [the longest x1 1.9 us: per_device(): jnp.einsum('thd,hrd->htr', value_heads, grad_value_b, preferred_element_t...]
    pallas_call x0 -> x5, Pallas kernels: none -> 17.9 us  [call(): pl.pallas_call(kernel, out_shape=out_shape, in_specs=specs, out_specs=jax...]
    unnamed x4 -> x0, waiting for transfers between devices: 16.4 us -> none
    all_to_all x0 -> x1, blocking collectives: none -> 15 us  [per_device(): back = lax.all_to_all(send, HEAD, 0, 0, tiled=True)]
    ppermute x4 -> x6, waiting for transfers between devices: 0.01 us -> 12.3 us  [shifted(): lax.ppermute(block, SEQ, [(i, (i + shift) % seqs) for i in range(seqs)])]
  transfers between devices with their start and end apart: 7 -> 7, of which waited for: 3 -> 3; matrix products, arithmetic and copies ran while one was open for 8% -> 4% of each run, Pallas kernels for 0% -> 0%
where the time goes in v1:
time: 73.1 us; the launch traced here: 72.7 us
  waiting for transfers between devices  19.9 us (27%)
  Pallas kernels  17.9 us (24%)
  blocking collectives  15 us (21%)
  starting transfers between devices  13.6 us (19%)
  local copies, waits for them, and re-layouts  4.95 us (7%)
    pallas_call x5, Pallas kernels, call(): pl.pallas_call(kernel, out_shape=out_shape, in_specs=specs, out_specs=jax...  17.9 us
    all_to_all x1, blocking collectives, per_device(): back = lax.all_to_all(send, HEAD, 0, 0, tiled=True)  15 us
    ppermute x6, waiting for transfers between devices, shifted(): lax.ppermute(block, SEQ, [(i, (i + shift) % seqs) for i in range(seqs)])  12.3 us
    ppermute x6, starting transfers between devices, shifted(): lax.ppermute(block, SEQ, [(i, (i + shift) % seqs) for i in range(seqs)])  8.44 us
    all_to_all x1, waiting for transfers between devices, per_device(): x = lax.all_to_all(packed, HEAD, 0, 0, tiled=True).reshape(count, width)  7.65 us
    all_to_all x1, starting transfers between devices, per_device(): x = lax.all_to_all(packed, HEAD, 0, 0, tiled=True).reshape(count, width)  5.2 us
    unnamed x20, local copies, waits for them, and re-layouts  2.81 us
  transfers between devices with their start and end apart: 7, of which 3 were waited for; matrix products, arithmetic and copies ran while one was open for 4% of the time, Pallas kernels for 0%

profile of v1, /device:TPU:0, one launch (start us, length us, event | category | flops | bytes accessed | tf_op | source)
XLA Modules:
  0.0 72.7 jit_solution(11259153891914734975)
XLA Ops:
  0.6 2.3 %pack.1 = bf16[8,128,256]{2,1,0:T(8,128)(2,1)} custom-call(bf16[128,512]{1,0:T(8,128)(2,1)} %q_ref.1, bf16[128,512]{1,0:T(8,128)(2,1)} %k_ref.1, bf16[128,512]{1,0:T(8,128)(2,1)} %v_ref.1, bf16[128,512]{1,0:T(8,128)(2,1)} %g_ref.1), custom_call_target="tpu_custom_call" | custom-call | tf_op jit(solution)/shard_map/pack/pallas_call | solution.py:358
  2.9 5.2 %all-to-all-start = ((bf16[8,128,256]{2,1,0:T(8,128)(2,1)}), bf16[8,128,256]{2,1,0:T(8,128)(2,1)S(1)}, u32[]{:S(2)}, u32[]{:S(2)}) async-start(bf16[8,128,256]{2,1,0:T(8,128)(2,1)} %pack.1), calls=%async_computation | async-start | bytes 1048576 | tf_op jit(solution)/shard_map/all_to_all | solution.py:393
  8.1 0.6 pad_add_fusion.h_ref.refs_0_
  8.7 0.6 constant_dynamic-slice_fusion.w_ref.refs_6_
  9.3 7.6 %all-to-all-done = bf16[8,128,256]{2,1,0:T(8,128)(2,1)S(1)} async-done(((bf16[8,128,256]{2,1,0:T(8,128)(2,1)}), bf16[8,128,256]{2,1,0:T(8,128)(2,1)S(1)}, u32[]{:S(2)}, u32[]{:S(2)}) %all-to-all-start) | async-done | bytes 524320 | tf_op jit(solution)/shard_map/all_to_all | solution.py:393
  17.0 0.8 %copy-done.1 = bf16[8,128,256]{2,1,0:T(8,128)(2,1)} copy-done((bf16[8,128,256]{2,1,0:T(8,128)(2,1)}, bf16[8,128,256]{2,1,0:T(8,128)(2,1)S(1)}, u32[]{:S(2)}) %copy-start.1) | copy-done | bytes 524312
  17.8 2.6 %local_sums.1 = (bf16[144,256]{1,0:T(8,128)(2,1)}, bf16[144,384]{1,0:T(8,128)(2,1)}, bf16[144,384]{1,0:T(8,128)(2,1)}, bf16[1024,256]{1,0:T(8,128)(2,1)}) custom-call(s32[2]{0:T(128)} %pad_add_fusion.h_ref.refs_0_, bf16[1024,256]{1,0:T(8,128)(2,1)} %bitcast.2, bf16[1,64,256]{2,1,0:T(8,128)(2,1)} %constant_dynamic-slice_fusion.w_ref.refs_6_), custom_call_target="tpu_custom_call" | custom-call | tf_op jit(solution)/shard_map/local_sums/pallas_call | solution.py:358
  20.3 1.6 %collective-permute-start = (bf16[144,384]{1,0:T(8,128)(2,1)}, bf16[144,384]{1,0:T(8,128)(2,1)S(1)}, u32[]{:S(2)}, u32[]{:S(2)}) collective-permute-start(bf16[144,384]{1,0:T(8,128)(2,1)} %get-tuple-element.23), channel_id=1, source_target_pairs={{0,8},{8,16},{16,24},{24,0},{1,9},{9,17},{17,25},{25,1},{2,10},{10... | collective-permute-start | bytes 331784 | tf_op jit(solution)/shard_map/ppermute | solution.py:406
  21.9 2.2 %collective-permute-start.2 = (bf16[144,384]{1,0:T(8,128)(2,1)}, bf16[144,384]{1,0:T(8,128)(2,1)S(1)}, u32[]{:S(2)}, u32[]{:S(2)}) collective-permute-start(bf16[144,384]{1,0:T(8,128)(2,1)} %get-tuple-element.24), channel_id=1, source_target_pairs={{0,24},{8,0},{16,8},{24,16},{1,25},{9,1},{17,9},{25,17},{2,26},{10... | collective-permute-start | bytes 331784 | tf_op jit(solution)/shard_map/ppermute | solution.py:406
  24.2 0.8 %collective-permute-start.1 = (bf16[144,256]{1,0:T(8,128)(2,1)}, bf16[144,256]{1,0:T(8,128)(2,1)S(1)}, u32[]{:S(2)}, u32[]{:S(2)}) collective-permute-start(bf16[144,256]{1,0:T(8,128)(2,1)} %get-tuple-element.22.refs_2_), channel_id=1, source_target_pairs={{0,16},{8,24},{16,0},{24,8},{1,17},{9,25},{17,1},{25,9},{2,18},{10... | collective-permute-start | bytes 221192 | tf_op jit(solution)/shard_map/ppermute | solution.py:406
  25.0 0.8 %reshape.24.refs_6_.refs_7_ = f32[128,1]{1,0:T(8,128)} reshape(f32[2,64]{1,0:T(2,128)S(1)} %copy-done.8) | data formatting | bytes 1024 | tf_op jit(solution)/shard_map/reshape | solution.py:412
  25.7 0.8 %reshape.25.refs_7_ = f32[128,1]{1,0:T(8,128)} reshape(f32[2,64]{1,0:T(2,128)S(1)} %copy-done.9) | data formatting | bytes 1024 | tf_op jit(solution)/shard_map/reshape | solution.py:413
  26.5 6.0 %collective-permute-done.1.refs_4_ = bf16[144,256]{1,0:T(8,128)(2,1)S(1)} collective-permute-done((bf16[144,256]{1,0:T(8,128)(2,1)}, bf16[144,256]{1,0:T(8,128)(2,1)S(1)}, u32[]{:S(2)}, u32[]{:S(2)}) %collective-permute-start.1) | collective-permute-done | bytes 73760 | tf_op jit(solution)/shard_map/ppermute | solution.py:406
  32.5 0.6 copy-done.6
  33.1 0.0 copy-done.2
  33.1 0.6 copy-done.3
  33.8 7.4 %attention.1 = (bf16[1024,128]{1,0:T(8,128)(2,1)}, f32[128,1024]{1,0:T(8,128)}, bf16[128,256]{1,0:T(8,128)(2,1)}, bf16[128,384]{1,0:T(8,128)(2,1)}, bf16[128,384]{1,0:T(8,128)(2,1)}, /*index=5*/f32[264,256]{1,0:T(8,128)}) custom-call(s32[2]{0:T(128)} %pad_add_fusion.h_ref.refs_0_, bf16[1024,256]{1,0:T(8,128)(2,1)} %bitcast.3, ...), custom_call_target="tpu_custom_call" | custom-call | tf_op jit(solution)/shard_map/attention/pallas_call | solution.py:358
  41.1 3.8 %collective-permute-start.5 = (bf16[128,384]{1,0:T(8,128)(2,1)}, bf16[128,384]{1,0:T(8,128)(2,1)S(1)}, u32[]{:S(2)}, u32[]{:S(2)}) collective-permute-start(bf16[128,384]{1,0:T(8,128)(2,1)} %get-tuple-element.27), channel_id=1, source_target_pairs={{0,24},{8,0},{16,8},{24,16},{1,25},{9,1},{17,9},{25,17},{2,26},{10... | collective-permute-start | bytes 294920 | tf_op jit(solution)/shard_map/ppermute | solution.py:406
  45.0 6.3 %collective-permute-done.4.refs_3_ = bf16[128,256]{1,0:T(8,128)(2,1)S(1)} collective-permute-done((bf16[128,256]{1,0:T(8,128)(2,1)}, bf16[128,256]{1,0:T(8,128)(2,1)S(1)}, u32[]{:S(2)}, u32[]{:S(2)}) %collective-permute-start.4) | collective-permute-done | bytes 65568 | tf_op jit(solution)/shard_map/ppermute | solution.py:406
  51.3 0.6 copy-done.7
  51.9 0.0 copy-done.4
  52.0 3.4 %landmark_backward.1 = bf16[8,160,256]{2,1,0:T(8,128)(2,1)} custom-call(s32[2]{0:T(128)} %pad_add_fusion.h_ref.refs_0_, bf16[128,256]{1,0:T(8,128)(2,1)} %get-tuple-element.25.refs_1_, bf16[128,384]{1,0:T(8,128)(2,1)} %copy-done.4, bf16[128,256]{1,0:T(8,128)(2,1)} %copy-done.7, bf16[128,384]{1,0:T(8,128)(2,1)} %copy-done.5, bf16[1024,256]{1,0:T(8,128)(2,1)} %bitcast.4, ...), custom_call_target="tpu_custom_call" | custom-call | tf_op jit(solution)/shard_map/landmark_backward/pallas_call | solution.py:358
  55.4 15.0 %all_to_all.10.r_ref = bf16[8,160,256]{2,1,0:T(8,128)(2,1)} all-to-all(bf16[8,160,256]{2,1,0:T(8,128)(2,1)} %landmark_backward.1), channel_id=1, replica_groups=mesh['seq'=4,'sub'=2,'half'=1,'part'=4] {'sub','part'}, dimensions={0} | all-to-all | bytes 1310720 | tf_op jit(solution)/shard_map/all_to_all | solution.py:467
  70.4 2.3 %unpack.1 = (bf16[128,512]{1,0:T(8,128)(2,1)}, bf16[128,512]{1,0:T(8,128)(2,1)}, bf16[128,512]{1,0:T(8,128)(2,1)}, bf16[128,512]{1,0:T(8,128)(2,1)}, f32[4,64]{1,0:T(4,128)}, /*index=5*/f32[1,8,64,64]{3,2,1,0:T(8,128)}) custom-call(bf16[8,160,256]{2,1,0:T(8,128)(2,1)} %all_to_all.10.r_ref), custom_call_target="tpu_custom_call" | custom-call | tf_op jit(solution)/shard_map/unpack/pallas_call | solution.py:358
  (20 shorter events, 0.1 us)
Async XLA Ops:
  0.6 8.1 %copy-start = (bf16[8,64,256]{2,1,0:T(8,128)(2,1)S(1)}, bf16[8,64,256]{2,1,0:T(8,128)(2,1)}, u32[]{:S(2)}) copy-start(bf16[8,64,256]{2,1,0:T(8,128)(2,1)} %param.10) | copy-start | bytes 786436
  2.9 14.1 %all-to-all-start = ((bf16[8,128,256]{2,1,0:T(8,128)(2,1)}), bf16[8,128,256]{2,1,0:T(8,128)(2,1)S(1)}, u32[]{:S(2)}, u32[]{:S(2)}) async-start(bf16[8,128,256]{2,1,0:T(8,128)(2,1)} %pack.1), calls=%async_computation | async-start | bytes 1048576 | tf_op jit(solution)/shard_map/all_to_all | solution.py:393
  17.0 0.8 %copy-start.1 = (bf16[8,128,256]{2,1,0:T(8,128)(2,1)}, bf16[8,128,256]{2,1,0:T(8,128)(2,1)S(1)}, u32[]{:S(2)}) copy-start(bf16[8,128,256]{2,1,0:T(8,128)(2,1)S(1)} %all-to-all-done) | copy-start | bytes 1572868
  20.3 12.1 %collective-permute-start = (bf16[144,384]{1,0:T(8,128)(2,1)}, bf16[144,384]{1,0:T(8,128)(2,1)S(1)}, u32[]{:S(2)}, u32[]{:S(2)}) collective-permute-start(bf16[144,384]{1,0:T(8,128)(2,1)} %get-tuple-element.23), channel_id=1, source_target_pairs={{0,8},{8,16},{16,24},{24,0},{1,9},{9,17},{17,25},{25,1},{2,10},{10... | collective-permute-start | bytes 331784 | tf_op jit(solution)/shard_map/ppermute | solution.py:406
  21.9 3.0 %copy-start.8 = (f32[2,64]{1,0:T(2,128)S(1)}, f32[2,64]{1,0:T(2,128)}, u32[]{:S(2)}) copy-start(f32[2,64]{1,0:T(2,128)} %param.11) | copy-start | bytes 1540
  21.9 10.5 %collective-permute-start.2 = (bf16[144,384]{1,0:T(8,128)(2,1)}, bf16[144,384]{1,0:T(8,128)(2,1)S(1)}, u32[]{:S(2)}, u32[]{:S(2)}) collective-permute-start(bf16[144,384]{1,0:T(8,128)(2,1)} %get-tuple-element.24), channel_id=1, source_target_pairs={{0,24},{8,0},{16,8},{24,16},{1,25},{9,1},{17,9},{25,17},{2,26},{10... | collective-permute-start | bytes 331784 | tf_op jit(solution)/shard_map/ppermute | solution.py:406
  24.2 1.6 %copy-start.9 = (f32[2,64]{1,0:T(2,128)S(1)}, f32[2,64]{1,0:T(2,128)}, u32[]{:S(2)}) copy-start(f32[2,64]{1,0:T(2,128)} %param.12) | copy-start | bytes 1540
  24.2 8.3 %collective-permute-start.1 = (bf16[144,256]{1,0:T(8,128)(2,1)}, bf16[144,256]{1,0:T(8,128)(2,1)S(1)}, u32[]{:S(2)}, u32[]{:S(2)}) collective-permute-start(bf16[144,256]{1,0:T(8,128)(2,1)} %get-tuple-element.22.refs_2_), channel_id=1, source_target_pairs={{0,16},{8,24},{16,0},{24,8},{1,17},{9,25},{17,1},{25,9},{2,18},{10... | collective-permute-start | bytes 221192 | tf_op jit(solution)/shard_map/ppermute | solution.py:406
  32.4 0.6 copy-start.6
  32.4 0.7 copy-start.2
  33.1 0.6 copy-start.3
  41.1 10.1 %collective-permute-start.3 = (bf16[128,384]{1,0:T(8,128)(2,1)}, bf16[128,384]{1,0:T(8,128)(2,1)S(1)}, u32[]{:S(2)}, u32[]{:S(2)}) collective-permute-start(bf16[128,384]{1,0:T(8,128)(2,1)} %get-tuple-element.26), channel_id=1, source_target_pairs={{0,8},{8,16},{16,24},{24,0},{1,9},{9,17},{17,25},{25,1},{2,10},{10... | collective-permute-start | bytes 294920 | tf_op jit(solution)/shard_map/ppermute | solution.py:406
  41.1 10.1 %collective-permute-start.5 = (bf16[128,384]{1,0:T(8,128)(2,1)}, bf16[128,384]{1,0:T(8,128)(2,1)S(1)}, u32[]{:S(2)}, u32[]{:S(2)}) collective-permute-start(bf16[128,384]{1,0:T(8,128)(2,1)} %get-tuple-element.27), channel_id=1, source_target_pairs={{0,24},{8,0},{16,8},{24,16},{1,25},{9,1},{17,9},{25,17},{2,26},{10... | collective-permute-start | bytes 294920 | tf_op jit(solution)/shard_map/ppermute | solution.py:406
  45.0 6.3 %collective-permute-start.4 = (bf16[128,256]{1,0:T(8,128)(2,1)}, bf16[128,256]{1,0:T(8,128)(2,1)S(1)}, u32[]{:S(2)}, u32[]{:S(2)}) collective-permute-start(bf16[128,256]{1,0:T(8,128)(2,1)} %get-tuple-element.25.refs_1_), channel_id=1, source_target_pairs={{0,16},{8,24},{16,0},{24,8},{1,17},{9,25},{17,1},{25,9},{2,18},{10... | collective-permute-start | bytes 196616 | tf_op jit(solution)/shard_map/ppermute | solution.py:406
  51.3 0.6 copy-start.7
  51.3 0.7 copy-start.4
  51.3 0.7 copy-start.5

commit v2 on v1

v2 whole, which is shorter than its diff:
```python
import functools
import math

import jax
import jax.numpy as jnp
import numpy as np
from jax import lax
from jax.experimental import pallas as pl
from jax.experimental.pallas import tpu as pltpu
from jax.sharding import Mesh
from jax.sharding import PartitionSpec as P

WIN = 128
EXTRA = 8
EPS = 1e-05
NEG = -1e30
VMEM_LIMIT = 24 * 1024 * 1024
BF = jnp.bfloat16
F32 = jnp.float32

NN = (((1,), (0,)), ((), ()))
NT = (((1,), (1,)), ((), ()))
SEQ = ("seq", "half")
HEAD = ("sub", "part")


def dot(a, b, dims=NN):
    return lax.dot_general(a, b, dims, preferred_element_type=F32)


def lanes(shape):
    return lax.broadcasted_iota(jnp.int32, shape, 1)


def rows(shape):
    return lax.broadcasted_iota(jnp.int32, shape, 0)


def pack_kernel(q_ref, k_ref, v_ref, g_ref, o_ref, buffer_ref, sems):
    heads, _, width = o_ref.shape
    dh = width // 4
    copies = []
    for slot, ref in enumerate((k_ref, v_ref, q_ref, g_ref)):
        copy = pltpu.make_async_copy(ref, buffer_ref.at[slot], sems.at[slot])
        copy.start()
        copies.append(copy)
    for slot, copy in enumerate(copies):
        copy.wait()
        for h in range(heads):
            o_ref[h, :, slot * dh : (slot + 1) * dh] = buffer_ref[slot, :, h * dh : (h + 1) * dh]


def split_rows(total_rows, width, pieces):
    r = rows((total_rows, width))
    out = jnp.zeros((total_rows, width), F32)
    for index, piece in enumerate(pieces):
        out = jnp.where(r == index, piece, out)
    return out.astype(BF)


def bf_pieces(x, count):
    out = []
    for _ in range(count):
        piece = x.astype(BF).astype(F32)
        out.append(piece)
        x = x - piece
    return out


def widen_proj(w):
    return jnp.concatenate([w, jnp.zeros_like(w)], axis=0)


def local_sums_kernel(place_ref, x_ref, w_ref, mid_ref, *out_refs):
    expo_ref = out_refs[-1]
    pair = x_ref.shape[1] // 2
    kv = x_ref[:, :pair]
    logits = dot(kv, widen_proj(w_ref[place_ref[2]]))
    peak = jnp.max(logits, axis=0, keepdims=True)
    expo = jnp.exp(logits - peak)
    total = jnp.sum(expo, axis=0, keepdims=True)
    expo_b = expo.astype(BF)
    expo_ref[...] = expo_b
    sums = dot(kv.T, expo_b).astype(BF)
    marks = sums.shape[1]
    tail = split_rows(EXTRA, marks, bf_pieces(peak, 3) + bf_pieces(total, 2))
    targets = [(mid_ref, None)]
    if len(out_refs) == 3:
        count = x_ref.shape[0]
        targets += [(out_refs[0], kv[count - WIN :]), (out_refs[1], kv[:WIN])]
    for ref, halo in targets:
        ref[:pair, :marks] = sums
        ref[pair:, :marks] = tail
        if halo is not None:
            ref[:pair, marks:] = halo
            ref[pair:, marks:] = jnp.zeros((EXTRA, pair), BF)


def collect(own_ref, recv_refs, stack_ref, index, marks):
    count = len(recv_refs) + 1
    stack_ref[index] = own_ref[...]
    for shift, ref in enumerate(recv_refs, start=1):
        stack_ref[lax.rem(index + (count - shift), count)] = ref[:, :marks]


def as_column(ref):
    row = jnp.concatenate([ref[0:1, :], ref[1:2, :]], axis=1)
    size = row.shape[1]
    return jnp.sum(
        jnp.where(rows((size, size)) == lanes((size, size)), row, 0.0), axis=1, keepdims=True
    )


def spread(x, width):
    return jnp.concatenate([x] * (width // x.shape[1]), axis=1)


def row_max(x):
    return jnp.max(x, axis=1, keepdims=True)


def row_sum(x):
    return jnp.sum(x, axis=1, keepdims=True)


def window_forward_kernel(x_ref, gain_src, bias_src, early_ref, a_ref, at_ref, affine_ref, *, scale):
    count, width = x_ref.shape
    pair = width // 2
    dh = pair // 2
    segments = count // WIN
    low = lanes((WIN, pair)) < dh
    zero_b = jnp.zeros((WIN, pair), BF)
    for slot, src in enumerate((gain_src, bias_src)):
        affine_ref[slot * pair : (slot + 1) * pair] = jnp.broadcast_to(
            as_column(src), (pair, affine_ref.shape[1])
        )
    for s in range(segments):
        qg = x_ref[s * WIN : (s + 1) * WIN, pair:]
        q0 = jnp.where(low, (qg.astype(F32) * scale).astype(BF), zero_b)
        g0 = jnp.where(low, zero_b, qg)
        a = jnp.concatenate([q0, g0], axis=0)
        a_ref[2 * s * WIN : 2 * (s + 1) * WIN] = a
        at_ref[s * pair : (s + 1) * pair] = a.T
        kvw = x_ref[max(s - 1, 0) * WIN : min(s + 2, segments) * WIN, :pair]
        sw = dot(a, kvw, NT)
        scores, grads = sw[:WIN], sw[WIN:]
        top = row_max(scores)
        expo = jnp.exp(scores - top)
        expo_b = expo.astype(BF)
        out = dot(expo_b, kvw)
        part = row_sum(expo_b.astype(F32) * grads)
        span = slice(s * WIN, (s + 1) * WIN)
        early_ref[span, :pair] = out
        for slot, stat in enumerate((top, row_sum(expo), part), start=1):
            early_ref[span, slot * pair : (slot + 1) * pair] = jnp.broadcast_to(stat, out.shape)


def landmark_forward_kernel(*refs, ring):
    lands = ring + 1 if ring else 3
    place_ref, early_ref, a_ref, at_ref = refs[:4]
    land_refs = refs[4 : 4 + lands]
    affine_ref = refs[4 + lands]
    outs = refs[5 + lands :]
    late_ref, rows_ref, mid_ref, plus_ref, minus_ref, stats_ref, *scratch = outs
    pair = mid_ref.shape[0]
    marks = mid_ref.shape[1]
    dh = pair // 2
    segments = early_ref.shape[0] // WIN
    z = place_ref[0]
    last = place_ref[1] - 1
    if ring:
        stack_ref = scratch[0]
        collect(land_refs[0], land_refs[1:], stack_ref, z, marks)
        halos = {0: land_refs[1][:pair, marks:], segments - 1: land_refs[-1][:pair, marks:]}
    else:
        stack_ref = land_refs[0]
        halos = {0: land_refs[1][...], segments - 1: land_refs[2][...]}
    groups = stack_ref.shape[0]

    peaks, totals = [], []
    for j in range(groups):
        tail = stack_ref[j, pair:, :].astype(F32)
        peaks.append(tail[0:1] + tail[1:2] + tail[2:3])
        totals.append(tail[3:4] + tail[4:5])
    peak = functools.reduce(jnp.maximum, peaks)
    total = jnp.zeros_like(peak)
    sums = jnp.zeros((pair, marks), F32)
    for j in range(groups):
        factor = jnp.exp(peaks[j] - peak)
        total = total + factor * totals[j]
        sums = sums + factor * stack_ref[j, :pair, :].astype(F32)
    inv_total = 1.0 / total
    mean = sums * inv_total
    normed, inverse = [], []
    for half in range(2):
        block = mean[half * dh : (half + 1) * dh]
        centred = block - jnp.mean(block, axis=0, keepdims=True)
        variance = jnp.mean(centred * centred, axis=0, keepdims=True)
        inv = 1.0 / jnp.sqrt(variance + EPS)
        normed.append(centred * inv)
        inverse.append(inv)
    normed = jnp.concatenate(normed, axis=0)
    land_f = normed * spread(affine_ref[:pair], marks) + spread(affine_ref[pair:], marks)
    land_t = land_f.astype(BF)
    land = land_f.T.astype(BF)
    own_tail = stack_ref[z, pair:, :].astype(F32)
    own_peak = own_tail[0:1] + own_tail[1:2] + own_tail[2:3]
    factor = jnp.exp(own_peak - peak) * inv_total
    stats_ref[:pair] = normed
    stats_ref[pair : 2 * pair] = mean
    r8 = rows((8, marks))
    stats_ref[2 * pair :] = jnp.where(r8 == 0, inverse[0], jnp.where(r8 == 1, inverse[1], factor))

    land_grad = jnp.zeros((pair, marks), F32)
    halo_grads = {}
    low = lanes((WIN, pair)) < dh
    for s in range(segments):
        span = slice(s * WIN, (s + 1) * WIN)
        a = a_ref[2 * s * WIN : 2 * (s + 1) * WIN]
        early, top_e, sum_e, part_e = (
            early_ref[span, slot * pair : (slot + 1) * pair] for slot in range(4)
        )
        sl = dot(a, land_t)
        scores, grads = sl[:WIN], sl[WIN:]
        top = jnp.maximum(row_max(scores), top_e)
        if s in halos:
            sh = dot(a, halos[s], NT)
            outside = z == (0 if s == 0 else last)
            scores_h, grads_h = jnp.where(outside, NEG, sh[:WIN]), sh[WIN:]
            top = jnp.maximum(top, row_max(scores_h))
        expo = jnp.exp(scores - spread(top, marks))
        scale_e = jnp.exp(top_e - top)
        total_row = row_sum(expo) + sum_e * scale_e
        part = part_e * scale_e
        out = early * scale_e
        if s in halos:
            expo_h = jnp.exp(scores_h - top)
            total_row = total_row + row_sum(expo_h)
            part = part + row_sum(expo_h.astype(BF).astype(F32) * grads_h)
        inv = 1.0 / total_row
        probs = expo * spread(inv, marks)
        probs_b = probs.astype(BF)
        delta = row_sum(probs_b.astype(F32) * grads) + part * inv
        b = jnp.concatenate([(probs * (grads - spread(delta, marks))).astype(BF), probs_b], axis=0)
        od = dot(b, land)
        at = at_ref[s * pair : (s + 1) * pair]
        if s in halos:
            probs_h = expo_h * inv
            b_h = jnp.concatenate(
                [(probs_h * (grads_h - delta)).astype(BF), probs_h.astype(BF)], axis=0
            )
            od = od + dot(b_h, halos[s])
            halo_grads[s] = dot(at, b_h).astype(BF)
        late_ref[span] = jnp.where(low, od[:WIN], od[WIN:] + out * inv)
        rows_ref[span, :pair] = top + jnp.log(total_row)
        rows_ref[span, pair:] = delta
        land_grad = land_grad + dot(at, b)
    land_b = land_grad.astype(BF)
    mid_ref[...] = land_b
    if ring:
        plus_ref[:, :marks] = land_b
        minus_ref[:, :marks] = land_b
        plus_ref[:, marks:] = halo_grads[segments - 1]
        minus_ref[:, marks:] = halo_grads[0]
    else:
        plus_ref[...] = halo_grads[segments - 1]
        minus_ref[...] = halo_grads[0]


def window_backward_kernel(x_ref, a_ref, at_ref, late_ref, rows_ref, od_ref, dkvt_ref, *, scale):
    count, width = x_ref.shape
    pair = width // 2
    dh = pair // 2
    segments = count // WIN
    dkvt_ref[...] = jnp.zeros(dkvt_ref.shape, F32)
    low = lanes((WIN, pair)) < dh
    for s in range(segments):
        span = slice(s * WIN, (s + 1) * WIN)
        near = slice(max(s - 1, 0) * WIN, min(s + 2, segments) * WIN)
        a = a_ref[2 * s * WIN : 2 * (s + 1) * WIN]
        kvw = x_ref[near, :pair]
        reach = near.stop - near.start
        sw = dot(a, kvw, NT)
        probs = jnp.exp(sw[:WIN] - spread(rows_ref[span, :pair], reach))
        grad_b = (probs * (sw[WIN:] - spread(rows_ref[span, pair:], reach))).astype(BF)
        late = late_ref[span]
        dq = (dot(grad_b, kvw) + late) * scale
        od_ref[span] = jnp.where(low, dq, late).astype(BF)
        b = jnp.concatenate([grad_b, probs.astype(BF)], axis=0)
        dkvt_ref[:, near] += dot(at_ref[s * pair : (s + 1) * pair], b)


def final_kernel(*refs, ring, sub, parts, tiled):
    grads_in = ring + 1 if ring else 1
    place_ref = refs[0]
    grad_refs = refs[1 : 1 + grads_in]
    rest = refs[1 + grads_in :]
    if ring:
        prev_src, next_src = grad_refs[1], grad_refs[-1]
    else:
        prev_src, next_src, *rest = rest
    x_ref, w_ref, affine_ref, expo_ref, od_ref, dkvt_ref, stats_ref, *outs = rest
    send_ref = outs[0]
    count, width = x_ref.shape
    pair = width // 2
    dh = pair // 2
    marks = expo_ref.shape[1]
    if ring:
        stack_ref = outs[-1]
        collect(grad_refs[0], grad_refs[1:], stack_ref, place_ref[0], marks)
    else:
        stack_ref = grad_refs[0]
    z = place_ref[0]
    from_prev = prev_src[:, prev_src.shape[1] - pair :].astype(F32)
    from_next = next_src[:, next_src.shape[1] - pair :].astype(F32)
    from_prev = jnp.where(z == 0, 0.0, from_prev)
    from_next = jnp.where(z == place_ref[1] - 1, 0.0, from_next)
    grad = stack_ref[0].astype(F32)
    for j in range(1, stack_ref.shape[0]):
        grad = grad + stack_ref[j].astype(F32)
    normed = stats_ref[:pair]
    mean = stats_ref[pair : 2 * pair]
    factor = stats_ref[2 * pair + 2 : 2 * pair + 3]
    gained = grad * spread(affine_ref[:pair], marks)
    blocks = []
    for half in range(2):
        part = slice(half * dh, (half + 1) * dh)
        g = gained[part]
        first = jnp.mean(g, axis=0, keepdims=True)
        second = jnp.mean(g * normed[part], axis=0, keepdims=True)
        inv = stats_ref[2 * pair + half : 2 * pair + half + 1]
        blocks.append(inv * (g - first - normed[part] * second))
    grad_mean = jnp.concatenate(blocks, axis=0)
    grad_b = grad_mean.astype(BF)
    column = jnp.sum(grad_b.astype(F32) * mean, axis=0, keepdims=True)
    scaled = (grad_mean * factor).astype(BF)

    gain_sum = jnp.sum(grad * normed, axis=1, keepdims=True)
    bias_sum = jnp.sum(grad, axis=1, keepdims=True)
    lane = lanes((pair, pair))
    square = jnp.where(lane == 0, gain_sum, jnp.where(lane == 1, bias_sum, 0.0)).T
    norm_hi = square[:8].astype(BF)
    norm_lo = (square[:8] - norm_hi.astype(F32)).astype(BF)
    norm_rows = jnp.concatenate(
        [
            jnp.concatenate([norm_hi, norm_lo], axis=1),
        ],
        axis=0,
    )

    kv = x_ref[:, :pair]
    wide = widen_proj(w_ref[place_ref[2]])
    expo_b = expo_ref[...]
    weights = expo_b.astype(F32) * factor
    grad_logit = (weights * (dot(kv, grad_b) - column)).astype(BF)
    land = dot(expo_b, scaled, NT) + dot(grad_logit, wide, NT)
    window = dkvt_ref[...].T
    dests, out_rows, _ = send_ref.shape
    step = count // dests
    dkv = land + window
    head_fix = from_prev.T
    tail_fix = from_next.T
    for d in range(dests):
        span = slice(d * step, (d + 1) * step)
        block = dkv[span]
        fix_top = head_fix if d == 0 else None
        fix_end = tail_fix if d == dests - 1 else None
        for at in range(0, step, WIN):
            piece = block[at : at + WIN]
            if fix_top is not None and at == 0:
                piece = piece + fix_top
            if fix_end is not None and at + WIN == step:
                piece = piece + fix_end
            send_ref[d, at : at + WIN, :pair] = piece.astype(BF)
        send_ref[d, :step, pair:] = od_ref[span]
        send_ref[d, out_rows - 8 :] = norm_rows
    kvt = kv.T
    group = count // sub
    for sb in range(sub):
        span = slice(sb * group, (sb + 1) * group)
        proj = dot(kvt[:, span], grad_logit[span])[:dh]
        if tiled:
            wide_part = marks // parts
            quarter = dh // 4
            for i in range(parts):
                tile = proj[:, i * wide_part : (i + 1) * wide_part].astype(BF)
                for k in range(4):
                    send_ref[
                        sb * parts + i, step : out_rows - 8, k * dh : (k + 1) * dh
                    ] = tile[k * quarter : (k + 1) * quarter]
        else:
            outs[1][...] = proj


def unpack_kernel(r_ref, att_ref, dq_ref, dk_ref, dv_ref, norm_ref, *proj_refs):
    heads, _, width = r_ref.shape
    dh = width // 4
    pair = 2 * dh
    step = att_ref.shape[0]
    for h in range(heads):
        cols = slice(h * dh, (h + 1) * dh)
        for slot, ref in enumerate((dk_ref, dv_ref, dq_ref, att_ref)):
            ref[:, cols] = r_ref[h, :step, slot * dh : (slot + 1) * dh]
    norm = jnp.zeros((8, pair), F32)
    for h in range(heads):
        block = r_ref[h, r_ref.shape[1] - 8 :, :].astype(F32)
        norm = norm + (block[:, :pair] + block[:, pair:])
    norm_ref[0:1] = norm[0:1, :dh]
    norm_ref[1:2] = norm[1:2, :dh]
    norm_ref[2:3] = norm[0:1, dh:]
    norm_ref[3:4] = norm[1:2, dh:]
    if proj_refs:
        proj_ref = proj_refs[0]
        quarter = dh // 4
        for h in range(heads):
            for k in range(4):
                proj_ref[0, h, k * quarter : (k + 1) * quarter] = r_ref[
                    h, step : r_ref.shape[1] - 8, k * dh : (k + 1) * dh
                ].astype(F32)


def shape_of(shape, dtype):
    return jax.ShapeDtypeStruct(shape, dtype)


VM = pl.BlockSpec(memory_space=pltpu.VMEM)
SM = pl.BlockSpec(memory_space=pltpu.SMEM)
ANY = pl.BlockSpec(memory_space=pltpu.HBM)


def call(kernel, out_shape, args, specs, name, scratch=(), keep=True, flops=0):
    args = [
        arg if spec is SM else pltpu.with_memory_space_constraint(arg, spec.memory_space)
        for arg, spec in zip(args, specs)
    ]
    if keep:
        out_shape = jax.tree.map(lambda s: pltpu.VMEM(s.shape, s.dtype), out_shape)
    cost = pl.CostEstimate(flops=flops, bytes_accessed=0, transcendentals=0) if flops else None
    return pl.pallas_call(
        kernel,
        out_shape=out_shape,
        in_specs=specs,
        out_specs=jax.tree.map(lambda _: VM, out_shape),
        scratch_shapes=scratch,
        compiler_params=pltpu.CompilerParams(vmem_limit_bytes=VMEM_LIMIT),
        cost_estimate=cost,
        name=name,
    )(*args)


def per_device(queries, keys, values, w_proj, ln_gain, ln_bias, cotangent):
    tokens_dev, features = queries.shape
    heads, dh, marks = w_proj.shape
    pair = 2 * dh
    width = 4 * dh
    count = tokens_dev * heads
    scale = 1.0 / math.sqrt(dh)
    seqs = lax.axis_size(SEQ)
    sub = lax.axis_size("sub")
    parts = lax.axis_size("part")
    halves = lax.axis_size("half")
    head = lax.axis_index(HEAD).astype(jnp.int32)
    z = lax.axis_index(SEQ).astype(jnp.int32)
    place = jnp.stack([z, jnp.int32(seqs), head])
    ring = seqs - 1 if 3 <= seqs <= 8 else 0
    wide_part = marks // parts
    tiled = halves == 1 and wide_part == dh and dh % 64 == 0

    packed = call(
        pack_kernel,
        shape_of((heads, tokens_dev, width), BF),
        (queries, keys, values, cotangent),
        [ANY] * 4,
        "pack",
        [pltpu.VMEM((4, tokens_dev, features), BF), pltpu.SemaphoreType.DMA((4,))],
    )
    x = lax.all_to_all(packed, HEAD, 0, 0, tiled=True).reshape(count, width)

    rows_out = pair + EXTRA
    out_shape = [shape_of((rows_out, marks), BF)]
    if ring:
        out_shape += [shape_of((rows_out, marks + pair), BF)] * 2
    out_shape.append(shape_of((count, marks), BF))
    mid, *halo_outs, expo = call(
        local_sums_kernel, out_shape, (place, x, w_proj), [SM, VM, VM], "local_sums"
    )

    def shifted(block, shift):
        return lax.ppermute(block, SEQ, [(i, (i + shift) % seqs) for i in range(seqs)])

    def forward(block, shift):
        route = [(i, i + shift) for i in range(seqs) if 0 <= i + shift < seqs]
        return lax.ppermute(block, SEQ, route)

    if ring:
        recv = [shifted(halo_outs[0], 1)]
        recv += [shifted(mid, k) for k in range(2, ring)]
        recv += [shifted(halo_outs[1], ring)]
        lands = [mid, *recv]
        halos = [recv[0], recv[-1]]
    else:
        halos = [forward(x[count - WIN :, :pair], 1), forward(x[:WIN, :pair], -1)]
        lands = [lax.all_gather(mid, SEQ), *halos]
    halo_wide = marks + pair if ring else pair
    work = 2 * count * 3 * WIN * pair
    early, a_all, at_all, affine = call(
        functools.partial(window_forward_kernel, scale=scale),
        [
            shape_of((count, 4 * pair), F32),
            shape_of((2 * count, pair), BF),
            shape_of((count // WIN * pair, 2 * WIN), BF),
            shape_of((2 * pair, pair), F32),
        ],
        (x, ln_gain, ln_bias),
        [VM] * 3,
        "window_forward",
        flops=3 * work,
    )
    late, row_stats, grad_mid, plus, minus, stats = call(
        functools.partial(landmark_forward_kernel, ring=ring),
        [
            shape_of((count, pair), F32),
            shape_of((count, 2 * pair), F32),
            shape_of((pair, marks), BF),
            shape_of((pair, halo_wide), BF),
            shape_of((pair, halo_wide), BF),
            shape_of((2 * pair + 8, marks), F32),
        ],
        (place, early, a_all, at_all, *lands, affine),
        [SM] + [VM] * (len(lands) + 4),
        "landmark_forward",
        [pltpu.VMEM((seqs, rows_out, marks), BF)] if ring else [],
    )
    if ring:
        grads = [grad_mid, shifted(plus, 1)]
        grads += [shifted(grad_mid, k) for k in range(2, ring)]
        grads += [shifted(minus, ring)]
    else:
        grads = [lax.all_gather(grad_mid, SEQ), forward(plus, 1), forward(minus, -1)]
    od, dkvt = call(
        functools.partial(window_backward_kernel, scale=scale),
        [shape_of((count, pair), BF), shape_of((pair, count), F32)],
        (x, a_all, at_all, late, row_stats),
        [VM] * 5,
        "window_backward",
        flops=5 * work,
    )
    send_rows = tokens_dev + 8 + (dh // 4 if tiled else 0)
    out_shape = [shape_of((heads, send_rows, width), BF)]
    if not tiled:
        out_shape.append(shape_of((dh, marks), F32))
    send, *proj = call(
        functools.partial(
            final_kernel, ring=ring, sub=sub if tiled else 1, parts=parts, tiled=tiled
        ),
        out_shape,
        (place, *grads, x, w_proj, affine, expo, od, dkvt, stats),
        [SM] + [VM] * (len(grads) + 7),
        "landmark_backward",
        [pltpu.VMEM((seqs, pair, marks), BF)] if ring else [],
    )
    back = lax.all_to_all(send, HEAD, 0, 0, tiled=True)
    out_shape = [shape_of((tokens_dev, features), BF)] * 4 + [shape_of((4, dh), F32)]
    if tiled:
        out_shape.append(shape_of((1, heads, dh, wide_part), F32))
    attended, dq, dk, dv, grad_norm, *tiles = call(
        unpack_kernel, out_shape, (back,), [VM], "unpack", keep=False
    )
    if tiled:
        grad_proj = tiles[0]
    else:
        full = lax.all_gather(proj[0], HEAD)
        inner = ("half", "part") if halves > 1 else "part"
        grad_proj = lax.psum_scatter(full, inner, scatter_dimension=2, tiled=True)[None] / parts
    return (attended, dq, dk, dv, grad_proj, grad_norm)


def solution(mesh):
    ctx, inner = mesh.shape["ctx"], mesh.shape["inner"]

    def whole(queries, keys, values, w_proj, ln_gain, ln_bias, cotangent):
        heads = w_proj.shape[0]
        part = min(heads, inner)
        sub = heads // part
        order = np.asarray(mesh.devices).reshape(ctx // sub, sub, inner // part, part)
        split = Mesh(order, ("seq", "sub", "half", "part"))
        every = P(("seq", "sub", "half", "part"), None)
        return jax.shard_map(
            per_device,
            mesh=split,
            in_specs=(every, every, every, P(), P(), P(), every),
            out_specs=(
                every,
                every,
                every,
                every,
                P(("seq", "sub"), None, None, ("half", "part")),
                P(),
            ),
            check_vma=False,
        )(queries, keys, values, w_proj, ln_gain, ln_bias, cotangent)

    return whole
```

time: 73.1 us -> 59.5 us (0.81)
  local copies, waits for them, and re-layouts: 4.95 us -> 0.01 us
  Pallas kernels: 17.9 us -> 14.2 us
  waiting for transfers between devices: 19.9 us -> 17.4 us
  blocking collectives: 15 us -> 13.1 us
    pallas_call x5 -> x7, Pallas kernels: 17.9 us -> 14.2 us  [call(): pl.pallas_call(kernel, out_shape=out_shape, in_specs=specs, out_specs=jax...]
    ppermute x6, waiting for transfers between devices: 12.3 us -> 8.58 us  [shifted(): lax.ppermute(block, SEQ, [(i, (i + shift) % seqs) for i in range(seqs)])]
    unnamed x20 -> x6, local copies, waits for them, and re-layouts: 2.81 us -> 0.01 us
    all_to_all x1, blocking collectives: 15 us -> 13.1 us  [per_device(): back = lax.all_to_all(send, HEAD, 0, 0, tiled=True)]
    reshape x2 -> x0, local copies, waits for them, and re-layouts: 1.52 us -> none  [the longest x1 0.76 us: per_device(): bias = ln_bias.reshape(pair, 1)]
    all_to_all x1, waiting for transfers between devices: 7.65 us -> 8.78 us  [per_device(): x = lax.all_to_all(packed, HEAD, 0, 0, tiled=True).reshape(count, width)]
  transfers between devices with their start and end apart: 7 -> 7, of which waited for: 3 -> 3; matrix products, arithmetic and copies ran while one was open for 4% -> 0% of each run, Pallas kernels for 0% -> 7%
where the time goes in v2:
time: 59.5 us; the launch traced here: 59.2 us
  waiting for transfers between devices  17.4 us (29%)
  Pallas kernels  14.2 us (24%)
  starting transfers between devices  13.7 us (23%)
  blocking collectives  13.1 us (22%)
  between operations  0.72 us (1%)
    pallas_call x7, Pallas kernels, call(): pl.pallas_call(kernel, out_shape=out_shape, in_specs=specs, out_specs=jax...  14.2 us
    all_to_all x1, blocking collectives, per_device(): back = lax.all_to_all(send, HEAD, 0, 0, tiled=True)  13.1 us
    all_to_all x1, waiting for transfers between devices, per_device(): x = lax.all_to_all(packed, HEAD, 0, 0, tiled=True).reshape(count, width)  8.78 us
    ppermute x6, waiting for transfers between devices, shifted(): lax.ppermute(block, SEQ, [(i, (i + shift) % seqs) for i in range(seqs)])  8.58 us
    ppermute x6, starting transfers between devices, shifted(): lax.ppermute(block, SEQ, [(i, (i + shift) % seqs) for i in range(seqs)])  8.54 us
    all_to_all x1, starting transfers between devices, per_device(): x = lax.all_to_all(packed, HEAD, 0, 0, tiled=True).reshape(count, width)  5.21 us
  transfers between devices with their start and end apart: 7, of which 3 were waited for; matrix products, arithmetic and copies ran while one was open for 0% of the time, Pallas kernels for 7%

profile of v2, /device:TPU:0, one launch (start us, length us, event | category | flops | bytes accessed | tf_op | source)
XLA Modules:
  0.0 59.2 jit_solution(9417493941213811376)
XLA Ops:
  0.6 0.0 copy-start
  0.7 2.3 %pack.1 = bf16[8,128,256]{2,1,0:T(8,128)(2,1)} custom-call(bf16[128,512]{1,0:T(8,128)(2,1)} %q_ref.1, bf16[128,512]{1,0:T(8,128)(2,1)} %k_ref.1, bf16[128,512]{1,0:T(8,128)(2,1)} %v_ref.1, bf16[128,512]{1,0:T(8,128)(2,1)} %g_ref.1), custom_call_target="tpu_custom_call" | custom-call | tf_op jit(solution)/shard_map/pack/pallas_call | solution.py:439
  3.0 5.2 %all-to-all-start = ((bf16[8,128,256]{2,1,0:T(8,128)(2,1)}), bf16[8,128,256]{2,1,0:T(8,128)(2,1)S(1)}, u32[]{:S(2)}, u32[]{:S(2)}) async-start(bf16[8,128,256]{2,1,0:T(8,128)(2,1)} %pack.1), calls=%async_computation | async-start | bytes 1048576 | tf_op jit(solution)/shard_map/all_to_all | solution.py:477
  8.2 0.1 pad_add_fusion.place_ref.refs_0_
  8.3 8.8 %all-to-all-done = bf16[8,128,256]{2,1,0:T(8,128)(2,1)S(1)} async-done(((bf16[8,128,256]{2,1,0:T(8,128)(2,1)}), bf16[8,128,256]{2,1,0:T(8,128)(2,1)S(1)}, u32[]{:S(2)}, u32[]{:S(2)}) %all-to-all-start) | async-done | bytes 524320 | tf_op jit(solution)/shard_map/all_to_all | solution.py:477
  17.0 1.3 %local_sums.1 = (bf16[136,256]{1,0:T(8,128)(2,1)S(1)}, bf16[136,384]{1,0:T(8,128)(2,1)S(1)}, bf16[136,384]{1,0:T(8,128)(2,1)S(1)}, bf16[1024,256]{1,0:T(8,128)(2,1)S(1)}) custom-call(s32[3]{0:T(128)S(1)} %pad_add_fusion.place_ref.refs_0_, bf16[1024,256]{1,0:T(8,128)(2,1)S(1)} %bitcast.3, bf16[8,64,256]{2,1,0:T(8,128)(2,1)S(1)} %copy-done), custom_call_target="tpu_custom_call" | custom-call | tf_op jit(solution)/shard_map/local_sums/pallas_call | solution.py:439
  18.4 1.6 %collective-permute-start = (bf16[136,384]{1,0:T(8,128)(2,1)S(1)}, bf16[136,384]{1,0:T(8,128)(2,1)S(1)}, u32[]{:S(2)}, u32[]{:S(2)}) collective-permute-start(bf16[136,384]{1,0:T(8,128)(2,1)S(1)} %get-tuple-element.32), channel_id=1, source_target_pairs={{0,8},{8,16},{16,24},{24,0},{1,9},{9,17},{17,25},{25,1},{2,10},{10... | collective-permute-start | bytes 313352 | tf_op jit(solution)/shard_map/ppermute | solution.py:489
  20.0 2.3 %collective-permute-start.2 = (bf16[136,384]{1,0:T(8,128)(2,1)S(1)}, bf16[136,384]{1,0:T(8,128)(2,1)S(1)}, u32[]{:S(2)}, u32[]{:S(2)}) collective-permute-start(bf16[136,384]{1,0:T(8,128)(2,1)S(1)} %get-tuple-element.33), channel_id=1, source_target_pairs={{0,24},{8,0},{16,8},{24,16},{1,25},{9,1},{17,9},{25,17},{2,26},{10... | collective-permute-start | bytes 313352 | tf_op jit(solution)/shard_map/ppermute | solution.py:489
  22.3 0.8 %collective-permute-start.1 = (bf16[136,256]{1,0:T(8,128)(2,1)S(1)}, bf16[136,256]{1,0:T(8,128)(2,1)S(1)}, u32[]{:S(2)}, u32[]{:S(2)}) collective-permute-start(bf16[136,256]{1,0:T(8,128)(2,1)S(1)} %get-tuple-element.31.refs_4_), channel_id=1, source_target_pairs={{0,16},{8,24},{16,0},{24,8},{1,17},{9,25},{17,1},{25,9},{2,18},{10... | collective-permute-start | bytes 208904 | tf_op jit(solution)/shard_map/ppermute | solution.py:489
  23.1 2.2 %window_forward.1 = (f32[1024,512]{1,0:T(8,128)S(1)}, bf16[2048,128]{1,0:T(8,128)(2,1)S(1)}, bf16[1024,256]{1,0:T(8,128)(2,1)S(1)}, f32[256,128]{1,0:T(8,128)S(1)}) custom-call(bf16[1024,256]{1,0:T(8,128)(2,1)S(1)} %bitcast.4, f32[2,64]{1,0:T(2,128)S(1)} %copy-done.1, f32[2,64]{1,0:T(2,128)S(1)} %copy-done.2), custom_call_target="tpu_custom_call" | custom-call | flops 301989888 | tf_op jit(solution)/shard_map/window_forward/pallas_call | solution.py:439
  25.3 4.6 %collective-permute-done.1.refs_6_ = bf16[136,256]{1,0:T(8,128)(2,1)S(1)} collective-permute-done((bf16[136,256]{1,0:T(8,128)(2,1)S(1)}, bf16[136,256]{1,0:T(8,128)(2,1)S(1)}, u32[]{:S(2)}, u32[]{:S(2)}) %collective-permute-start.1) | collective-permute-done | bytes 69664 | tf_op jit(solution)/shard_map/ppermute | solution.py:489
  29.9 0.0 collective-permute-done.refs_5_
  29.9 0.0 collective-permute-done.2.refs_7_
  29.9 3.6 %landmark_forward.1 = (f32[1024,128]{1,0:T(8,128)S(1)}, f32[1024,256]{1,0:T(8,128)S(1)}, bf16[128,256]{1,0:T(8,128)(2,1)S(1)}, bf16[128,384]{1,0:T(8,128)(2,1)S(...) custom-call(s32[3]{0:T(128)S(1)} %pad_add_fusion.place_ref.refs_0_, f32[1024,512]{1,0:T(8,128)S(1)} %get-tuple-element.28.refs_1_, ...), custom_call_target="tpu_custom_call" | custom-call | tf_op jit(solution)/shard_map/landmark_forward/pallas_call | solution.py:439
  33.6 0.1 collective-permute-start.3
  33.6 3.8 %collective-permute-start.5 = (bf16[128,384]{1,0:T(8,128)(2,1)S(1)}, bf16[128,384]{1,0:T(8,128)(2,1)S(1)}, u32[]{:S(2)}, u32[]{:S(2)}) collective-permute-start(bf16[128,384]{1,0:T(8,128)(2,1)S(1)} %get-tuple-element.37), channel_id=1, source_target_pairs={{0,24},{8,0},{16,8},{24,16},{1,25},{9,1},{17,9},{25,17},{2,26},{10... | collective-permute-start | bytes 294920 | tf_op jit(solution)/shard_map/ppermute | solution.py:489
  37.4 0.0 collective-permute-start.4
  37.4 2.1 %window_backward.1 = (bf16[1024,128]{1,0:T(8,128)(2,1)S(1)}, f32[128,1024]{1,0:T(8,128)S(1)}) custom-call(bf16[1024,256]{1,0:T(8,128)(2,1)S(1)} %bitcast.5, bf16[2048,128]{1,0:T(8,128)(2,1)S(1)} %get-tuple-element.29.refs_2_.a_ref, bf16[1024,256]{1,0:T(8,128)(2,1)S(1)} %get-tuple-element.30.refs_3_.at_ref, f32[1024,128]{1,0:T(8,128)S(1)} %get-tuple-element.39.late_ref, ...), custom_call_target="tpu_custom_call" | custom-call | flops 503316480 | tf_op jit(solution)/shard_map/window_backward/pallas_call | solution.py:439
  39.6 3.9 %collective-permute-done.4.refs_3_ = bf16[128,256]{1,0:T(8,128)(2,1)S(1)} collective-permute-done((bf16[128,256]{1,0:T(8,128)(2,1)S(1)}, bf16[128,256]{1,0:T(8,128)(2,1)S(1)}, u32[]{:S(2)}, u32[]{:S(2)}) %collective-permute-start.4) | collective-permute-done | bytes 65568 | tf_op jit(solution)/shard_map/ppermute | solution.py:489
  43.5 0.0 collective-permute-done.3.refs_2_
  43.5 0.0 collective-permute-done.5.refs_4_
  43.5 1.4 %landmark_backward.1 = bf16[8,152,256]{2,1,0:T(8,128)(2,1)S(1)} custom-call(s32[3]{0:T(128)S(1)} %pad_add_fusion.place_ref.refs_0_, bf16[128,256]{1,0:T(8,128)(2,1)S(1)} %get-tuple-element.35.refs_1_, bf16[128,384]{1,0:T(8,128)(2,1)S(1)} %collective-permute-done.3.refs_2_, bf16[128,256]{1,0:T(8,128)(2,1)S(1)} %collective-permute-done.4.refs_3_, ...), custom_call_target="tpu_custom_call" | custom-call | tf_op jit(solution)/shard_map/landmark_backward/pallas_call | solution.py:439
  44.9 13.1 %all_to_all.10.r_ref = bf16[8,152,256]{2,1,0:T(8,128)(2,1)S(1)} all-to-all(bf16[8,152,256]{2,1,0:T(8,128)(2,1)S(1)} %landmark_backward.1), channel_id=1, replica_groups=mesh['seq'=4,'sub'=2,'half'=1,'part'=4] {'sub','part'}, dimensions={0} | all-to-all | bytes 1245184 | tf_op jit(solution)/shard_map/all_to_all | solution.py:562
  58.0 1.2 %unpack.1 = (bf16[128,512]{1,0:T(8,128)(2,1)}, bf16[128,512]{1,0:T(8,128)(2,1)}, bf16[128,512]{1,0:T(8,128)(2,1)}, bf16[128,512]{1,0:T(8,128)(2,1)}, f32[4,64]{1,0:T(4,128)}, /*index=5*/f32[1,8,64,64]{3,2,1,0:T(8,128)}) custom-call(bf16[8,152,256]{2,1,0:T(8,128)(2,1)S(1)} %all_to_all.10.r_ref), custom_call_target="tpu_custom_call" | custom-call | tf_op jit(solution)/shard_map/unpack/pallas_call | solution.py:439
  (5 shorter events, 0.0 us)
Async XLA Ops:
  0.6 16.4 %copy-start = (bf16[8,64,256]{2,1,0:T(8,128)(2,1)S(1)}, bf16[8,64,256]{2,1,0:T(8,128)(2,1)}, u32[]{:S(2)}) copy-start(bf16[8,64,256]{2,1,0:T(8,128)(2,1)} %refs_6_.1) | copy-start | bytes 786436
  0.6 22.4 %copy-start.2 = (f32[2,64]{1,0:T(2,128)S(1)}, f32[2,64]{1,0:T(2,128)}, u32[]{:S(2)}) copy-start(f32[2,64]{1,0:T(2,128)} %bias_src.1) | copy-start | bytes 1540
  0.7 22.4 %copy-start.1 = (f32[2,64]{1,0:T(2,128)S(1)}, f32[2,64]{1,0:T(2,128)}, u32[]{:S(2)}) copy-start(f32[2,64]{1,0:T(2,128)} %gain_src.1) | copy-start | bytes 1540
  3.0 14.1 %all-to-all-start = ((bf16[8,128,256]{2,1,0:T(8,128)(2,1)}), bf16[8,128,256]{2,1,0:T(8,128)(2,1)S(1)}, u32[]{:S(2)}, u32[]{:S(2)}) async-start(bf16[8,128,256]{2,1,0:T(8,128)(2,1)} %pack.1), calls=%async_computation | async-start | bytes 1048576 | tf_op jit(solution)/shard_map/all_to_all | solution.py:477
  18.4 11.5 %collective-permute-start = (bf16[136,384]{1,0:T(8,128)(2,1)S(1)}, bf16[136,384]{1,0:T(8,128)(2,1)S(1)}, u32[]{:S(2)}, u32[]{:S(2)}) collective-permute-start(bf16[136,384]{1,0:T(8,128)(2,1)S(1)} %get-tuple-element.32), channel_id=1, source_target_pairs={{0,8},{8,16},{16,24},{24,0},{1,9},{9,17},{17,25},{25,1},{2,10},{10... | collective-permute-start | bytes 313352 | tf_op jit(solution)/shard_map/ppermute | solution.py:489
  20.0 9.9 %collective-permute-start.2 = (bf16[136,384]{1,0:T(8,128)(2,1)S(1)}, bf16[136,384]{1,0:T(8,128)(2,1)S(1)}, u32[]{:S(2)}, u32[]{:S(2)}) collective-permute-start(bf16[136,384]{1,0:T(8,128)(2,1)S(1)} %get-tuple-element.33), channel_id=1, source_target_pairs={{0,24},{8,0},{16,8},{24,16},{1,25},{9,1},{17,9},{25,17},{2,26},{10... | collective-permute-start | bytes 313352 | tf_op jit(solution)/shard_map/ppermute | solution.py:489
  22.3 7.6 %collective-permute-start.1 = (bf16[136,256]{1,0:T(8,128)(2,1)S(1)}, bf16[136,256]{1,0:T(8,128)(2,1)S(1)}, u32[]{:S(2)}, u32[]{:S(2)}) collective-permute-start(bf16[136,256]{1,0:T(8,128)(2,1)S(1)} %get-tuple-element.31.refs_4_), channel_id=1, source_target_pairs={{0,16},{8,24},{16,0},{24,8},{1,17},{9,25},{17,1},{25,9},{2,18},{10... | collective-permute-start | bytes 208904 | tf_op jit(solution)/shard_map/ppermute | solution.py:489
  33.6 9.9 %collective-permute-start.3 = (bf16[128,384]{1,0:T(8,128)(2,1)S(1)}, bf16[128,384]{1,0:T(8,128)(2,1)S(1)}, u32[]{:S(2)}, u32[]{:S(2)}) collective-permute-start(bf16[128,384]{1,0:T(8,128)(2,1)S(1)} %get-tuple-element.36), channel_id=1, source_target_pairs={{0,8},{8,16},{16,24},{24,0},{1,9},{9,17},{17,25},{25,1},{2,10},{10... | collective-permute-start | bytes 294920 | tf_op jit(solution)/shard_map/ppermute | solution.py:489
  33.6 9.9 %collective-permute-start.5 = (bf16[128,384]{1,0:T(8,128)(2,1)S(1)}, bf16[128,384]{1,0:T(8,128)(2,1)S(1)}, u32[]{:S(2)}, u32[]{:S(2)}) collective-permute-start(bf16[128,384]{1,0:T(8,128)(2,1)S(1)} %get-tuple-element.37), channel_id=1, source_target_pairs={{0,24},{8,0},{16,8},{24,16},{1,25},{9,1},{17,9},{25,17},{2,26},{10... | collective-permute-start | bytes 294920 | tf_op jit(solution)/shard_map/ppermute | solution.py:489
  37.4 6.1 %collective-permute-start.4 = (bf16[128,256]{1,0:T(8,128)(2,1)S(1)}, bf16[128,256]{1,0:T(8,128)(2,1)S(1)}, u32[]{:S(2)}, u32[]{:S(2)}) collective-permute-start(bf16[128,256]{1,0:T(8,128)(2,1)S(1)} %get-tuple-element.35.refs_1_), channel_id=1, source_target_pairs={{0,16},{8,24},{16,0},{24,8},{1,17},{9,25},{17,1},{25,9},{2,18},{10... | collective-permute-start | bytes 196616 | tf_op jit(solution)/shard_map/ppermute | solution.py:489

commit v3 on v2

--- a/solution.py
+++ b/solution.py
@@ -14,6 +14,7 @@
 EXTRA = 8
 EPS = 1e-05
 NEG = -1e30
+BATCH = 8
 VMEM_LIMIT = 24 * 1024 * 1024
 BF = jnp.bfloat16
 F32 = jnp.float32
@@ -36,9 +37,10 @@
     return lax.broadcasted_iota(jnp.int32, shape, 0)
 
 
-def pack_kernel(q_ref, k_ref, v_ref, g_ref, o_ref, buffer_ref, sems):
+def pack_kernel(z_ref, head_ref, q_ref, k_ref, v_ref, g_ref, o_ref, buffer_ref, sems):
     heads, _, width = o_ref.shape
     dh = width // 4
+    del z_ref, head_ref
     copies = []
     for slot, ref in enumerate((k_ref, v_ref, q_ref, g_ref)):
         copy = pltpu.make_async_copy(ref, buffer_ref.at[slot], sems.at[slot])
@@ -71,11 +73,11 @@
     return jnp.concatenate([w, jnp.zeros_like(w)], axis=0)
 
 
-def local_sums_kernel(place_ref, x_ref, w_ref, mid_ref, *out_refs):
+def local_sums_kernel(head_ref, x_ref, w_ref, mid_ref, *out_refs):
     expo_ref = out_refs[-1]
     pair = x_ref.shape[1] // 2
     kv = x_ref[:, :pair]
-    logits = dot(kv, widen_proj(w_ref[place_ref[2]]))
+    logits = dot(kv, widen_proj(w_ref[head_ref[0]]))
     peak = jnp.max(logits, axis=0, keepdims=True)
     expo = jnp.exp(logits - peak)
     total = jnp.sum(expo, axis=0, keepdims=True)
@@ -140,7 +142,7 @@
         g0 = jnp.where(low, zero_b, qg)
         a = jnp.concatenate([q0, g0], axis=0)
         a_ref[2 * s * WIN : 2 * (s + 1) * WIN] = a
-        at_ref[s * pair : (s + 1) * pair] = a.T
+        at_ref[:, 2 * s * WIN : 2 * (s + 1) * WIN] = a.T
         kvw = x_ref[max(s - 1, 0) * WIN : min(s + 2, segments) * WIN, :pair]
         sw = dot(a, kvw, NT)
         scores, grads = sw[:WIN], sw[WIN:]
@@ -148,16 +150,16 @@
         expo = jnp.exp(scores - top)
         expo_b = expo.astype(BF)
         out = dot(expo_b, kvw)
-        part = row_sum(expo_b.astype(F32) * grads)
+        part = row_sum(expo * grads)
         span = slice(s * WIN, (s + 1) * WIN)
         early_ref[span, :pair] = out
         for slot, stat in enumerate((top, row_sum(expo), part), start=1):
             early_ref[span, slot * pair : (slot + 1) * pair] = jnp.broadcast_to(stat, out.shape)
 
 
-def landmark_forward_kernel(*refs, ring):
+def landmark_forward_kernel(*refs, ring, seqs):
     lands = ring + 1 if ring else 3
-    place_ref, early_ref, a_ref, at_ref = refs[:4]
+    z_ref, early_ref, a_ref, at_ref = refs[:4]
     land_refs = refs[4 : 4 + lands]
     affine_ref = refs[4 + lands]
     outs = refs[5 + lands :]
@@ -166,8 +168,8 @@
     marks = mid_ref.shape[1]
     dh = pair // 2
     segments = early_ref.shape[0] // WIN
-    z = place_ref[0]
-    last = place_ref[1] - 1
+    z = z_ref[0]
+    last = seqs - 1
     if ring:
         stack_ref = scratch[0]
         collect(land_refs[0], land_refs[1:], stack_ref, z, marks)
@@ -184,77 +186,92 @@
         totals.append(tail[3:4] + tail[4:5])
     peak = functools.reduce(jnp.maximum, peaks)
     total = jnp.zeros_like(peak)
-    sums = jnp.zeros((pair, marks), F32)
-    for j in range(groups):
-        factor = jnp.exp(peaks[j] - peak)
-        total = total + factor * totals[j]
-        sums = sums + factor * stack_ref[j, :pair, :].astype(F32)
+    factors = [jnp.exp(p - peak) for p in peaks]
+    for factor, part in zip(factors, totals):
+        total = total + factor * part
     inv_total = 1.0 / total
-    mean = sums * inv_total
-    normed, inverse = [], []
+    factors = [factor * inv_total for factor in factors]
+    land_t, inverse = [], []
     for half in range(2):
-        block = mean[half * dh : (half + 1) * dh]
-        centred = block - jnp.mean(block, axis=0, keepdims=True)
-        variance = jnp.mean(centred * centred, axis=0, keepdims=True)
-        inv = 1.0 / jnp.sqrt(variance + EPS)
-        normed.append(centred * inv)
+        block = slice(half * dh, (half + 1) * dh)
+        mean = factors[0] * stack_ref[0, block, :].astype(F32)
+        for j in range(1, groups):
+            mean = mean + factors[j] * stack_ref[j, block, :].astype(F32)
+        stats_ref[pair + half * dh : pair + (half + 1) * dh] = mean
+        centred = mean - jnp.mean(mean, axis=0, keepdims=True)
+        inv = 1.0 / jnp.sqrt(jnp.mean(centred * centred, axis=0, keepdims=True) + EPS)
+        normed = centred * inv
+        stats_ref[block] = normed
         inverse.append(inv)
-    normed = jnp.concatenate(normed, axis=0)
-    land_f = normed * spread(affine_ref[:pair], marks) + spread(affine_ref[pair:], marks)
-    land_t = land_f.astype(BF)
-    land = land_f.T.astype(BF)
+        gain = affine_ref[half * dh : (half + 1) * dh]
+        bias = affine_ref[pair + half * dh : pair + (half + 1) * dh]
+        land_t.append((normed * spread(gain, marks) + spread(bias, marks)).astype(BF))
+    land_t = jnp.concatenate(land_t, axis=0)
+    land = land_t.T
     own_tail = stack_ref[z, pair:, :].astype(F32)
     own_peak = own_tail[0:1] + own_tail[1:2] + own_tail[2:3]
     factor = jnp.exp(own_peak - peak) * inv_total
-    stats_ref[:pair] = normed
-    stats_ref[pair : 2 * pair] = mean
     r8 = rows((8, marks))
     stats_ref[2 * pair :] = jnp.where(r8 == 0, inverse[0], jnp.where(r8 == 1, inverse[1], factor))
 
+    low = lanes((WIN, pair)) < dh
     land_grad = jnp.zeros((pair, marks), F32)
     halo_grads = {}
-    low = lanes((WIN, pair)) < dh
-    for s in range(segments):
-        span = slice(s * WIN, (s + 1) * WIN)
-        a = a_ref[2 * s * WIN : 2 * (s + 1) * WIN]
-        early, top_e, sum_e, part_e = (
-            early_ref[span, slot * pair : (slot + 1) * pair] for slot in range(4)
-        )
-        sl = dot(a, land_t)
-        scores, grads = sl[:WIN], sl[WIN:]
-        top = jnp.maximum(row_max(scores), top_e)
-        if s in halos:
-            sh = dot(a, halos[s], NT)
-            outside = z == (0 if s == 0 else last)
-            scores_h, grads_h = jnp.where(outside, NEG, sh[:WIN]), sh[WIN:]
-            top = jnp.maximum(top, row_max(scores_h))
-        expo = jnp.exp(scores - spread(top, marks))
-        scale_e = jnp.exp(top_e - top)
-        total_row = row_sum(expo) + sum_e * scale_e
-        part = part_e * scale_e
-        out = early * scale_e
-        if s in halos:
-            expo_h = jnp.exp(scores_h - top)
-            total_row = total_row + row_sum(expo_h)
-            part = part + row_sum(expo_h.astype(BF).astype(F32) * grads_h)
-        inv = 1.0 / total_row
-        probs = expo * spread(inv, marks)
-        probs_b = probs.astype(BF)
-        delta = row_sum(probs_b.astype(F32) * grads) + part * inv
-        b = jnp.concatenate([(probs * (grads - spread(delta, marks))).astype(BF), probs_b], axis=0)
-        od = dot(b, land)
-        at = at_ref[s * pair : (s + 1) * pair]
-        if s in halos:
-            probs_h = expo_h * inv
-            b_h = jnp.concatenate(
-                [(probs_h * (grads_h - delta)).astype(BF), probs_h.astype(BF)], axis=0
+    for first in range(0, segments, BATCH):
+        batch = range(first, min(first + BATCH, segments))
+        spans = {s: slice(s * WIN, (s + 1) * WIN) for s in batch}
+        blocks = {s: a_ref[2 * s * WIN : 2 * (s + 1) * WIN] for s in batch}
+        early = {
+            s: [early_ref[spans[s], slot * pair : (slot + 1) * pair] for slot in range(4)]
+            for s in batch
+        }
+        sl = {s: dot(blocks[s], land_t) for s in batch}
+        sh = {s: dot(blocks[s], halos[s], NT) for s in batch if s in halos}
+        scores = {s: sl[s][:WIN] for s in batch}
+        grads = {s: sl[s][WIN:] for s in batch}
+        scores_h = {
+            s: jnp.where(z == (0 if s == 0 else last), NEG, sh[s][:WIN]) for s in sh
+        }
+        top = {s: jnp.maximum(row_max(scores[s]), early[s][1]) for s in batch}
+        for s in sh:
+            top[s] = jnp.maximum(top[s], row_max(scores_h[s]))
+        expo = {s: jnp.exp(scores[s] - spread(top[s], marks)) for s in batch}
+        expo_h = {s: jnp.exp(scores_h[s] - top[s]) for s in sh}
+        scale_e = {s: jnp.exp(early[s][1] - top[s]) for s in batch}
+        total_row, part = {}, {}
+        for s in batch:
+            total_row[s] = row_sum(expo[s]) + early[s][2] * scale_e[s]
+            part[s] = row_sum(expo[s] * grads[s]) + early[s][3] * scale_e[s]
+            if s in sh:
+                total_row[s] = total_row[s] + row_sum(expo_h[s])
+                part[s] = part[s] + row_sum(expo_h[s] * sh[s][WIN:])
+        inv = {s: 1.0 / total_row[s] for s in batch}
+        delta = {s: part[s] * inv[s] for s in batch}
+        b, b_h = {}, {}
+        for s in batch:
+            probs = expo[s] * spread(inv[s], marks)
+            b[s] = jnp.concatenate(
+                [(probs * (grads[s] - spread(delta[s], marks))).astype(BF), probs.astype(BF)],
+                axis=0,
             )
-            od = od + dot(b_h, halos[s])
-            halo_grads[s] = dot(at, b_h).astype(BF)
-        late_ref[span] = jnp.where(low, od[:WIN], od[WIN:] + out * inv)
-        rows_ref[span, :pair] = top + jnp.log(total_row)
-        rows_ref[span, pair:] = delta
-        land_grad = land_grad + dot(at, b)
+            rows_ref[spans[s], :pair] = top[s] + jnp.log(total_row[s])
+            rows_ref[spans[s], pair:] = delta[s]
+        for s in sh:
+            probs = expo_h[s] * inv[s]
+            b_h[s] = jnp.concatenate(
+                [(probs * (sh[s][WIN:] - delta[s])).astype(BF), probs.astype(BF)], axis=0
+            )
+        for s in batch:
+            od = dot(b[s], land)
+            if s in sh:
+                od = od + dot(b_h[s], halos[s])
+            late_ref[spans[s]] = jnp.where(
+                low, od[:WIN], od[WIN:] + early[s][0] * (scale_e[s] * inv[s])
+            )
+        reach = slice(2 * batch[0] * WIN, 2 * (batch[-1] + 1) * WIN)
+        land_grad = land_grad + dot(at_ref[:, reach], jnp.concatenate([b[s] for s in batch], axis=0))
+        for s in sh:
+            halo_grads[s] = dot(at_ref[:, 2 * s * WIN : 2 * (s + 1) * WIN], b_h[s]).astype(BF)
     land_b = land_grad.astype(BF)
     mid_ref[...] = land_b
     if ring:
@@ -287,14 +304,14 @@
         dq = (dot(grad_b, kvw) + late) * scale
         od_ref[span] = jnp.where(low, dq, late).astype(BF)
         b = jnp.concatenate([grad_b, probs.astype(BF)], axis=0)
-        dkvt_ref[:, near] += dot(at_ref[s * pair : (s + 1) * pair], b)
-
-
-def final_kernel(*refs, ring, sub, parts, tiled):
+        dkvt_ref[:, near] += dot(at_ref[:, 2 * s * WIN : 2 * (s + 1) * WIN], b)
+
+
+def final_kernel(*refs, ring, seqs, sub, parts, tiled):
     grads_in = ring + 1 if ring else 1
-    place_ref = refs[0]
-    grad_refs = refs[1 : 1 + grads_in]
-    rest = refs[1 + grads_in :]
+    z_ref, head_ref = refs[:2]
+    grad_refs = refs[2 : 2 + grads_in]
+    rest = refs[2 + grads_in :]
     if ring:
         prev_src, next_src = grad_refs[1], grad_refs[-1]
     else:
@@ -307,14 +324,14 @@
     marks = expo_ref.shape[1]
     if ring:
         stack_ref = outs[-1]
-        collect(grad_refs[0], grad_refs[1:], stack_ref, place_ref[0], marks)
+        collect(grad_refs[0], grad_refs[1:], stack_ref, z_ref[0], marks)
     else:
         stack_ref = grad_refs[0]
-    z = place_ref[0]
+    z = z_ref[0]
     from_prev = prev_src[:, prev_src.shape[1] - pair :].astype(F32)
     from_next = next_src[:, next_src.shape[1] - pair :].astype(F32)
     from_prev = jnp.where(z == 0, 0.0, from_prev)
-    from_next = jnp.where(z == place_ref[1] - 1, 0.0, from_next)
+    from_next = jnp.where(z == seqs - 1, 0.0, from_next)
     grad = stack_ref[0].astype(F32)
     for j in range(1, stack_ref.shape[0]):
         grad = grad + stack_ref[j].astype(F32)
@@ -349,7 +366,7 @@
     )
 
     kv = x_ref[:, :pair]
-    wide = widen_proj(w_ref[place_ref[2]])
+    wide = widen_proj(w_ref[head_ref[0]])
     expo_b = expo_ref[...]
     weights = expo_b.astype(F32) * factor
     grad_logit = (weights * (dot(kv, grad_b) - column)).astype(BF)
@@ -461,7 +478,8 @@
     halves = lax.axis_size("half")
     head = lax.axis_index(HEAD).astype(jnp.int32)
     z = lax.axis_index(SEQ).astype(jnp.int32)
-    place = jnp.stack([z, jnp.int32(seqs), head])
+    z = z.reshape(1)
+    head = head.reshape(1)
     ring = seqs - 1 if 3 <= seqs <= 8 else 0
     wide_part = marks // parts
     tiled = halves == 1 and wide_part == dh and dh % 64 == 0
@@ -469,8 +487,8 @@
     packed = call(
         pack_kernel,
         shape_of((heads, tokens_dev, width), BF),
-        (queries, keys, values, cotangent),
-        [ANY] * 4,
+        (z, head, queries, keys, values, cotangent),
+        [SM] * 2 + [ANY] * 4,
         "pack",
         [pltpu.VMEM((4, tokens_dev, features), BF), pltpu.SemaphoreType.DMA((4,))],
     )
@@ -482,7 +500,7 @@
         out_shape += [shape_of((rows_out, marks + pair), BF)] * 2
     out_shape.append(shape_of((count, marks), BF))
     mid, *halo_outs, expo = call(
-        local_sums_kernel, out_shape, (place, x, w_proj), [SM, VM, VM], "local_sums"
+        local_sums_kernel, out_shape, (head, x, w_proj), [SM, VM, VM], "local_sums"
     )
 
     def shifted(block, shift):
@@ -508,7 +526,7 @@
         [
             shape_of((count, 4 * pair), F32),
             shape_of((2 * count, pair), BF),
-            shape_of((count // WIN * pair, 2 * WIN), BF),
+            shape_of((pair, 2 * count), BF),
             shape_of((2 * pair, pair), F32),
         ],
         (x, ln_gain, ln_bias),
@@ -517,7 +535,7 @@
         flops=3 * work,
     )
     late, row_stats, grad_mid, plus, minus, stats = call(
-        functools.partial(landmark_forward_kernel, ring=ring),
+        functools.partial(landmark_forward_kernel, ring=ring, seqs=seqs),
         [
             shape_of((count, pair), F32),
             shape_of((count, 2 * pair), F32),
@@ -526,7 +544,7 @@
             shape_of((pair, halo_wide), BF),
             shape_of((2 * pair + 8, marks), F32),
         ],
-        (place, early, a_all, at_all, *lands, affine),
+        (z, early, a_all, at_all, *lands, affine),
         [SM] + [VM] * (len(lands) + 4),
         "landmark_forward",
         [pltpu.VMEM((seqs, rows_out, marks), BF)] if ring else [],
@@ -551,11 +569,16 @@
         out_shape.append(shape_of((dh, marks), F32))
     send, *proj = call(
         functools.partial(
-            final_kernel, ring=ring, sub=sub if tiled else 1, parts=parts, tiled=tiled
+            final_kernel,
+            ring=ring,
+            seqs=seqs,
+            sub=sub if tiled else 1,
+            parts=parts,
+            tiled=tiled,
         ),
         out_shape,
-        (place, *grads, x, w_proj, affine, expo, od, dkvt, stats),
-        [SM] + [VM] * (len(grads) + 7),
+        (z, head, *grads, x, w_proj, affine, expo, od, dkvt, stats),
+        [SM, SM] + [VM] * (len(grads) + 7),
         "landmark_backward",
         [pltpu.VMEM((seqs, pair, marks), BF)] if ring else [],
     )

time: 59.5 us -> 56 us (0.941)
  blocking collectives: 13.1 us -> 27.2 us
  waiting for transfers between devices: 17.4 us -> 8.69 us
  starting transfers between devices: 13.7 us -> 8.54 us
  Pallas kernels: 14.2 us -> 10.7 us
    all_to_all x0 -> x1, blocking collectives: none -> 14 us  [per_device(): x = lax.all_to_all(packed, HEAD, 0, 0, tiled=True).reshape(count, width)]
    all_to_all x1 -> x0, waiting for transfers between devices: 8.78 us -> none  [per_device(): x = lax.all_to_all(packed, HEAD, 0, 0, tiled=True).reshape(count, width)]
    all_to_all x1 -> x0, starting transfers between devices: 5.21 us -> none  [per_device(): x = lax.all_to_all(packed, HEAD, 0, 0, tiled=True).reshape(count, width)]
    pallas_call x7, Pallas kernels: 14.2 us -> 10.7 us  [call(): pl.pallas_call(kernel, out_shape=out_shape, in_specs=specs, out_specs=jax...]
  transfers between devices with their start and end apart: 7 -> 6, of which waited for: 3 -> 2; matrix products, arithmetic and copies ran while one was open for 0% -> 0% of each run, Pallas kernels for 7% -> 8%
where the time goes in v3:
time: 56 us; the launch traced here: 55.8 us
  blocking collectives  27.2 us (49%)
  Pallas kernels  10.7 us (19%)
  waiting for transfers between devices  8.69 us (16%)
  starting transfers between devices  8.54 us (15%)
  between operations  0.72 us (1%)
    all_to_all x1, blocking collectives, per_device(): x = lax.all_to_all(packed, HEAD, 0, 0, tiled=True).reshape(count, width)  14 us
    all_to_all x1, blocking collectives, per_device(): back = lax.all_to_all(send, HEAD, 0, 0, tiled=True)  13.2 us
    pallas_call x7, Pallas kernels, call(): pl.pallas_call(kernel, out_shape=out_shape, in_specs=specs, out_specs=jax...  10.7 us
    ppermute x6, waiting for transfers between devices, shifted(): lax.ppermute(block, SEQ, [(i, (i + shift) % seqs) for i in range(seqs)])  8.69 us
    ppermute x6, starting transfers between devices, shifted(): lax.ppermute(block, SEQ, [(i, (i + shift) % seqs) for i in range(seqs)])  8.54 us
  transfers between devices with their start and end apart: 6, of which 2 were waited for; matrix products, arithmetic and copies ran while one was open for 0% of the time, Pallas kernels for 8%

profile of v3, /device:TPU:0, one launch (start us, length us, event | category | flops | bytes accessed | tf_op | source)
XLA Modules:
  0.0 55.8 jit_solution(7263185610725468745)
XLA Ops:
  0.6 0.0 copy-start
  0.6 0.0 copy-start.2
  0.7 0.0 copy-start.1
  0.7 1.5 %pack.1 = bf16[8,128,256]{2,1,0:T(8,128)(2,1)S(1)} custom-call(s32[1]{0:T(128)} %bitcast.z_ref.refs_0_, s32[1]{0:T(128)} %bitcast.1.head_ref.refs_1_, bf16[128,512]{1,0:T(8,128)(2,1)} %q_ref.1, bf16[128,512]{1,0:T(8,128)(2,1)} %k_ref.1, bf16[128,512]{1,0:T(8,128)(2,1)} %v_ref.1, bf16[128,512]{1,0:T(8,128)(2,1)} %g_ref.1), custom_call_target="tpu_custom_call" | custom-call | tf_op jit(solution)/shard_map/pack/pallas_call | solution.py:456
  2.2 14.0 %all_to_all.10 = bf16[8,128,256]{2,1,0:T(8,128)(2,1)S(1)} all-to-all(bf16[8,128,256]{2,1,0:T(8,128)(2,1)S(1)} %pack.1), channel_id=1, replica_groups=mesh['seq'=4,'sub'=2,'half'=1,'part'=4] {'sub','part'}, dimensions={0} | all-to-all | bytes 1048576 | tf_op jit(solution)/shard_map/all_to_all | solution.py:495
  16.2 0.8 %local_sums.1 = (bf16[136,256]{1,0:T(8,128)(2,1)S(1)}, bf16[136,384]{1,0:T(8,128)(2,1)S(1)}, bf16[136,384]{1,0:T(8,128)(2,1)S(1)}, bf16[1024,256]{1,0:T(8,128)(2,1)S(1)}) custom-call(s32[1]{0:T(128)} %bitcast.1.head_ref.refs_1_, bf16[1024,256]{1,0:T(8,128)(2,1)S(1)} %bitcast.3, bf16[8,64,256]{2,1,0:T(8,128)(2,1)S(1)} %copy-done), custom_call_target="tpu_custom_call" | custom-call | tf_op jit(solution)/shard_map/local_sums/pallas_call | solution.py:456
  17.0 1.6 %collective-permute-start = (bf16[136,384]{1,0:T(8,128)(2,1)S(1)}, bf16[136,384]{1,0:T(8,128)(2,1)S(1)}, u32[]{:S(2)}, u32[]{:S(2)}) collective-permute-start(bf16[136,384]{1,0:T(8,128)(2,1)S(1)} %get-tuple-element.32), channel_id=1, source_target_pairs={{0,8},{8,16},{16,24},{24,0},{1,9},{9,17},{17,25},{25,1},{2,10},{10... | collective-permute-start | bytes 313352 | tf_op jit(solution)/shard_map/ppermute | solution.py:507
  18.6 2.2 %collective-permute-start.2 = (bf16[136,384]{1,0:T(8,128)(2,1)S(1)}, bf16[136,384]{1,0:T(8,128)(2,1)S(1)}, u32[]{:S(2)}, u32[]{:S(2)}) collective-permute-start(bf16[136,384]{1,0:T(8,128)(2,1)S(1)} %get-tuple-element.33), channel_id=1, source_target_pairs={{0,24},{8,0},{16,8},{24,16},{1,25},{9,1},{17,9},{25,17},{2,26},{10... | collective-permute-start | bytes 313352 | tf_op jit(solution)/shard_map/ppermute | solution.py:507
  20.8 0.8 %collective-permute-start.1 = (bf16[136,256]{1,0:T(8,128)(2,1)S(1)}, bf16[136,256]{1,0:T(8,128)(2,1)S(1)}, u32[]{:S(2)}, u32[]{:S(2)}) collective-permute-start(bf16[136,256]{1,0:T(8,128)(2,1)S(1)} %get-tuple-element.31.refs_4_), channel_id=1, source_target_pairs={{0,16},{8,24},{16,0},{24,8},{1,17},{9,25},{17,1},{25,9},{2,18},{10... | collective-permute-start | bytes 208904 | tf_op jit(solution)/shard_map/ppermute | solution.py:507
  21.6 2.2 %window_forward.1 = (f32[1024,512]{1,0:T(8,128)S(1)}, bf16[2048,128]{1,0:T(8,128)(2,1)S(1)}, bf16[128,2048]{1,0:T(8,128)(2,1)S(1)}, f32[256,128]{1,0:T(8,128)S(1)}) custom-call(bf16[1024,256]{1,0:T(8,128)(2,1)S(1)} %bitcast.4, f32[2,64]{1,0:T(2,128)S(1)} %copy-done.1, f32[2,64]{1,0:T(2,128)S(1)} %copy-done.2), custom_call_target="tpu_custom_call" | custom-call | flops 301989888 | tf_op jit(solution)/shard_map/window_forward/pallas_call | solution.py:456
  23.8 4.7 %collective-permute-done.1.refs_6_ = bf16[136,256]{1,0:T(8,128)(2,1)S(1)} collective-permute-done((bf16[136,256]{1,0:T(8,128)(2,1)S(1)}, bf16[136,256]{1,0:T(8,128)(2,1)S(1)}, u32[]{:S(2)}, u32[]{:S(2)}) %collective-permute-start.1) | collective-permute-done | bytes 69664 | tf_op jit(solution)/shard_map/ppermute | solution.py:507
  28.6 0.0 collective-permute-done.refs_5_
  28.6 0.0 collective-permute-done.2.refs_7_
  28.6 1.9 %landmark_forward.1 = (f32[1024,128]{1,0:T(8,128)S(1)}, f32[1024,256]{1,0:T(8,128)S(1)}, bf16[128,256]{1,0:T(8,128)(2,1)S(1)}, bf16[128,384]{1,0:T(8,128)(2,1)S(...) custom-call(s32[1]{0:T(128)} %bitcast.z_ref.refs_0_, f32[1024,512]{1,0:T(8,128)S(1)} %get-tuple-element.28.refs_1_, ...), custom_call_target="tpu_custom_call" | custom-call | tf_op jit(solution)/shard_map/landmark_forward/pallas_call | solution.py:456
  30.5 0.1 collective-permute-start.3
  30.6 3.8 %collective-permute-start.5 = (bf16[128,384]{1,0:T(8,128)(2,1)S(1)}, bf16[128,384]{1,0:T(8,128)(2,1)S(1)}, u32[]{:S(2)}, u32[]{:S(2)}) collective-permute-start(bf16[128,384]{1,0:T(8,128)(2,1)S(1)} %get-tuple-element.37), channel_id=1, source_target_pairs={{0,24},{8,0},{16,8},{24,16},{1,25},{9,1},{17,9},{25,17},{2,26},{10... | collective-permute-start | bytes 294920 | tf_op jit(solution)/shard_map/ppermute | solution.py:507
  34.4 0.0 collective-permute-start.4
  34.4 2.1 %window_backward.1 = (bf16[1024,128]{1,0:T(8,128)(2,1)S(1)}, f32[128,1024]{1,0:T(8,128)S(1)}) custom-call(bf16[1024,256]{1,0:T(8,128)(2,1)S(1)} %bitcast.5, bf16[2048,128]{1,0:T(8,128)(2,1)S(1)} %get-tuple-element.29.refs_2_.a_ref, bf16[128,2048]{1,0:T(8,128)(2,1)S(1)} %get-tuple-element.30.refs_3_.at_ref, f32[1024,128]{1,0:T(8,128)S(1)} %get-tuple-element.39.late_ref, ...), custom_call_target="tpu_custom_call" | custom-call | flops 503316480 | tf_op jit(solution)/shard_map/window_backward/pallas_call | solution.py:456
  36.5 3.9 %collective-permute-done.4.refs_4_ = bf16[128,256]{1,0:T(8,128)(2,1)S(1)} collective-permute-done((bf16[128,256]{1,0:T(8,128)(2,1)S(1)}, bf16[128,256]{1,0:T(8,128)(2,1)S(1)}, u32[]{:S(2)}, u32[]{:S(2)}) %collective-permute-start.4) | collective-permute-done | bytes 65568 | tf_op jit(solution)/shard_map/ppermute | solution.py:507
  40.5 0.0 collective-permute-done.3.refs_3_
  40.5 0.0 collective-permute-done.5.refs_5_
  40.5 0.9 %landmark_backward.1 = bf16[8,152,256]{2,1,0:T(8,128)(2,1)S(1)} custom-call(s32[1]{0:T(128)} %bitcast.z_ref.refs_0_, s32[1]{0:T(128)} %bitcast.1.head_ref.refs_1_, bf16[128,256]{1,0:T(8,128)(2,1)S(1)} %get-tuple-element.35.refs_2_, bf16[128,384]{1,0:T(8,128)(2,1)S(1)} %collective-permute-done.3.refs_3_, bf16[128,256]{1,0:T(8,128)(2,1)S(1)} %collective-permute-done.4.refs_4_, ...), custom_call_target="tpu_custom_call" | custom-call | tf_op jit(solution)/shard_map/landmark_backward/pallas_call | solution.py:456
  41.4 13.2 %all_to_all.11.r_ref = bf16[8,152,256]{2,1,0:T(8,128)(2,1)S(1)} all-to-all(bf16[8,152,256]{2,1,0:T(8,128)(2,1)S(1)} %landmark_backward.1), channel_id=1, replica_groups=mesh['seq'=4,'sub'=2,'half'=1,'part'=4] {'sub','part'}, dimensions={0} | all-to-all | bytes 1245184 | tf_op jit(solution)/shard_map/all_to_all | solution.py:585
  54.7 1.2 %unpack.1 = (bf16[128,512]{1,0:T(8,128)(2,1)}, bf16[128,512]{1,0:T(8,128)(2,1)}, bf16[128,512]{1,0:T(8,128)(2,1)}, bf16[128,512]{1,0:T(8,128)(2,1)}, f32[4,64]{1,0:T(4,128)}, /*index=5*/f32[1,8,64,64]{3,2,1,0:T(8,128)}) custom-call(bf16[8,152,256]{2,1,0:T(8,128)(2,1)S(1)} %all_to_all.11.r_ref), custom_call_target="tpu_custom_call" | custom-call | tf_op jit(solution)/shard_map/unpack/pallas_call | solution.py:456
  (3 shorter events, 0.0 us)
Async XLA Ops:
  0.6 15.5 %copy-start = (bf16[8,64,256]{2,1,0:T(8,128)(2,1)S(1)}, bf16[8,64,256]{2,1,0:T(8,128)(2,1)}, u32[]{:S(2)}) copy-start(bf16[8,64,256]{2,1,0:T(8,128)(2,1)} %refs_7_.1) | copy-start | bytes 786436
  0.6 21.0 %copy-start.2 = (f32[2,64]{1,0:T(2,128)S(1)}, f32[2,64]{1,0:T(2,128)}, u32[]{:S(2)}) copy-start(f32[2,64]{1,0:T(2,128)} %bias_src.1) | copy-start | bytes 1540
  0.7 21.0 %copy-start.1 = (f32[2,64]{1,0:T(2,128)S(1)}, f32[2,64]{1,0:T(2,128)}, u32[]{:S(2)}) copy-start(f32[2,64]{1,0:T(2,128)} %gain_src.1) | copy-start | bytes 1540
  17.0 11.6 %collective-permute-start = (bf16[136,384]{1,0:T(8,128)(2,1)S(1)}, bf16[136,384]{1,0:T(8,128)(2,1)S(1)}, u32[]{:S(2)}, u32[]{:S(2)}) collective-permute-start(bf16[136,384]{1,0:T(8,128)(2,1)S(1)} %get-tuple-element.32), channel_id=1, source_target_pairs={{0,8},{8,16},{16,24},{24,0},{1,9},{9,17},{17,25},{25,1},{2,10},{10... | collective-permute-start | bytes 313352 | tf_op jit(solution)/shard_map/ppermute | solution.py:507
  18.6 10.0 %collective-permute-start.2 = (bf16[136,384]{1,0:T(8,128)(2,1)S(1)}, bf16[136,384]{1,0:T(8,128)(2,1)S(1)}, u32[]{:S(2)}, u32[]{:S(2)}) collective-permute-start(bf16[136,384]{1,0:T(8,128)(2,1)S(1)} %get-tuple-element.33), channel_id=1, source_target_pairs={{0,24},{8,0},{16,8},{24,16},{1,25},{9,1},{17,9},{25,17},{2,26},{10... | collective-permute-start | bytes 313352 | tf_op jit(solution)/shard_map/ppermute | solution.py:507
  20.8 7.7 %collective-permute-start.1 = (bf16[136,256]{1,0:T(8,128)(2,1)S(1)}, bf16[136,256]{1,0:T(8,128)(2,1)S(1)}, u32[]{:S(2)}, u32[]{:S(2)}) collective-permute-start(bf16[136,256]{1,0:T(8,128)(2,1)S(1)} %get-tuple-element.31.refs_4_), channel_id=1, source_target_pairs={{0,16},{8,24},{16,0},{24,8},{1,17},{9,25},{17,1},{25,9},{2,18},{10... | collective-permute-start | bytes 208904 | tf_op jit(solution)/shard_map/ppermute | solution.py:507
  30.5 9.9 %collective-permute-start.3 = (bf16[128,384]{1,0:T(8,128)(2,1)S(1)}, bf16[128,384]{1,0:T(8,128)(2,1)S(1)}, u32[]{:S(2)}, u32[]{:S(2)}) collective-permute-start(bf16[128,384]{1,0:T(8,128)(2,1)S(1)} %get-tuple-element.36), channel_id=1, source_target_pairs={{0,8},{8,16},{16,24},{24,0},{1,9},{9,17},{17,25},{25,1},{2,10},{10... | collective-permute-start | bytes 294920 | tf_op jit(solution)/shard_map/ppermute | solution.py:507
  30.6 9.9 %collective-permute-start.5 = (bf16[128,384]{1,0:T(8,128)(2,1)S(1)}, bf16[128,384]{1,0:T(8,128)(2,1)S(1)}, u32[]{:S(2)}, u32[]{:S(2)}) collective-permute-start(bf16[128,384]{1,0:T(8,128)(2,1)S(1)} %get-tuple-element.37), channel_id=1, source_target_pairs={{0,24},{8,0},{16,8},{24,16},{1,25},{9,1},{17,9},{25,17},{2,26},{10... | collective-permute-start | bytes 294920 | tf_op jit(solution)/shard_map/ppermute | solution.py:507
  34.4 6.1 %collective-permute-start.4 = (bf16[128,256]{1,0:T(8,128)(2,1)S(1)}, bf16[128,256]{1,0:T(8,128)(2,1)S(1)}, u32[]{:S(2)}, u32[]{:S(2)}) collective-permute-start(bf16[128,256]{1,0:T(8,128)(2,1)S(1)} %get-tuple-element.35.refs_2_), channel_id=1, source_target_pairs={{0,16},{8,24},{16,0},{24,8},{1,17},{9,25},{17,1},{25,9},{2,18},{10... | collective-permute-start | bytes 196616 | tf_op jit(solution)/shard_map/ppermute | solution.py:507

commit v4 on v3

--- a/solution.py
+++ b/solution.py
@@ -37,19 +37,42 @@
     return lax.broadcasted_iota(jnp.int32, shape, 0)
 
 
-def pack_kernel(z_ref, head_ref, q_ref, k_ref, v_ref, g_ref, o_ref, buffer_ref, sems):
-    heads, _, width = o_ref.shape
+def gather_pieces(piece_refs, stack_ref, head):
+    for k, ref in enumerate(piece_refs):
+        stack_ref[head ^ k] = ref[...]
+
+
+def scatter_pieces(stack_ref, piece_refs, head):
+    for k, ref in enumerate(piece_refs):
+        ref[...] = stack_ref[head ^ k]
+
+
+def pack_kernel(head_ref, z_ref, q_ref, k_ref, v_ref, g_ref, w_src, gain_src, bias_src, *rest):
+    *piece_refs, w_ref, gain_ref, bias_ref, stack_ref, buffer_ref, sems = rest
+    del z_ref
+    heads, _, width = stack_ref.shape
     dh = width // 4
-    del z_ref, head_ref
     copies = []
     for slot, ref in enumerate((k_ref, v_ref, q_ref, g_ref)):
         copy = pltpu.make_async_copy(ref, buffer_ref.at[slot], sems.at[slot])
         copy.start()
         copies.append(copy)
+    small = ((w_src.at[head_ref[0]], w_ref), (gain_src, gain_ref), (bias_src, bias_ref))
+    extra = [
+        pltpu.make_async_copy(src, dst, sems.at[len(copies) + slot])
+        for slot, (src, dst) in enumerate(small)
+    ]
+    for copy in extra:
+        copy.start()
     for slot, copy in enumerate(copies):
         copy.wait()
         for h in range(heads):
-            o_ref[h, :, slot * dh : (slot + 1) * dh] = buffer_ref[slot, :, h * dh : (h + 1) * dh]
+            stack_ref[h, :, slot * dh : (slot + 1) * dh] = buffer_ref[
+                slot, :, h * dh : (h + 1) * dh
+            ]
+    scatter_pieces(stack_ref, piece_refs, head_ref[0])
+    for copy in extra:
+        copy.wait()
 
 
 def split_rows(total_rows, width, pieces):
@@ -73,11 +96,14 @@
     return jnp.concatenate([w, jnp.zeros_like(w)], axis=0)
 
 
-def local_sums_kernel(head_ref, x_ref, w_ref, mid_ref, *out_refs):
-    expo_ref = out_refs[-1]
-    pair = x_ref.shape[1] // 2
-    kv = x_ref[:, :pair]
-    logits = dot(kv, widen_proj(w_ref[head_ref[0]]))
+def local_sums_kernel(head_ref, w_ref, *refs, heads):
+    x_ref, expo_ref, mid_ref, *halo_refs = refs[heads:]
+    gather_pieces(refs[:heads], x_ref, head_ref[0])
+    _, tokens_dev, width = x_ref.shape
+    count = heads * tokens_dev
+    pair = width // 2
+    kv = x_ref[:, :, :pair].reshape(count, pair)
+    logits = dot(kv, widen_proj(w_ref[...]))
     peak = jnp.max(logits, axis=0, keepdims=True)
     expo = jnp.exp(logits - peak)
     total = jnp.sum(expo, axis=0, keepdims=True)
@@ -87,9 +113,8 @@
     marks = sums.shape[1]
     tail = split_rows(EXTRA, marks, bf_pieces(peak, 3) + bf_pieces(total, 2))
     targets = [(mid_ref, None)]
-    if len(out_refs) == 3:
-        count = x_ref.shape[0]
-        targets += [(out_refs[0], kv[count - WIN :]), (out_refs[1], kv[:WIN])]
+    if halo_refs:
+        targets += [(halo_refs[0], kv[count - WIN :]), (halo_refs[1], kv[:WIN])]
     for ref, halo in targets:
         ref[:pair, :marks] = sums
         ref[pair:, :marks] = tail
@@ -307,7 +332,7 @@
         dkvt_ref[:, near] += dot(at_ref[:, 2 * s * WIN : 2 * (s + 1) * WIN], b)
 
 
-def final_kernel(*refs, ring, seqs, sub, parts, tiled):
+def final_kernel(*refs, ring, seqs, heads, sub, parts, tiled):
     grads_in = ring + 1 if ring else 1
     z_ref, head_ref = refs[:2]
     grad_refs = refs[2 : 2 + grads_in]
@@ -317,16 +342,17 @@
     else:
         prev_src, next_src, *rest = rest
     x_ref, w_ref, affine_ref, expo_ref, od_ref, dkvt_ref, stats_ref, *outs = rest
-    send_ref = outs[0]
     count, width = x_ref.shape
     pair = width // 2
     dh = pair // 2
     marks = expo_ref.shape[1]
     if ring:
-        stack_ref = outs[-1]
+        stack_ref = outs.pop()
         collect(grad_refs[0], grad_refs[1:], stack_ref, z_ref[0], marks)
     else:
         stack_ref = grad_refs[0]
+    send_ref = outs.pop()
+    piece_refs, proj_refs = outs[:heads], outs[heads:]
     z = z_ref[0]
     from_prev = prev_src[:, prev_src.shape[1] - pair :].astype(F32)
     from_next = next_src[:, next_src.shape[1] - pair :].astype(F32)
@@ -366,7 +392,7 @@
     )
 
     kv = x_ref[:, :pair]
-    wide = widen_proj(w_ref[head_ref[0]])
+    wide = widen_proj(w_ref[...])
     expo_b = expo_ref[...]
     weights = expo_b.astype(F32) * factor
     grad_logit = (weights * (dot(kv, grad_b) - column)).astype(BF)
@@ -406,10 +432,13 @@
                         sb * parts + i, step : out_rows - 8, k * dh : (k + 1) * dh
                     ] = tile[k * quarter : (k + 1) * quarter]
         else:
-            outs[1][...] = proj
-
-
-def unpack_kernel(r_ref, att_ref, dq_ref, dk_ref, dv_ref, norm_ref, *proj_refs):
+            proj_refs[0][...] = proj
+    scatter_pieces(send_ref, piece_refs, head_ref[0])
+
+
+def unpack_kernel(head_ref, *refs, heads):
+    att_ref, dq_ref, dk_ref, dv_ref, norm_ref, *proj_refs, r_ref = refs[heads:]
+    gather_pieces(refs[:heads], r_ref, head_ref[0])
     heads, _, width = r_ref.shape
     dh = width // 4
     pair = 2 * dh
@@ -484,24 +513,44 @@
     wide_part = marks // parts
     tiled = halves == 1 and wide_part == dh and dh % 64 == 0
 
-    packed = call(
+    def exchange(pieces):
+        out = dict(enumerate(pieces[:1]))
+        for k in reversed(range(1, heads)):
+            out[k] = lax.ppermute(pieces[k], HEAD, [(i, i ^ k) for i in range(heads)])
+        return [out[k] for k in range(heads)]
+
+    *packed, w_head, gain, bias = call(
         pack_kernel,
+        [shape_of((tokens_dev, width), BF)] * heads
+        + [shape_of((dh, marks), BF)]
+        + [shape_of((2, dh), F32)] * 2,
+        (head, z, queries, keys, values, cotangent, w_proj, ln_gain, ln_bias),
+        [SM] * 2 + [ANY] * 7,
+        "pack",
+        [
+            pltpu.VMEM((heads, tokens_dev, width), BF),
+            pltpu.VMEM((4, tokens_dev, features), BF),
+            pltpu.SemaphoreType.DMA((7,)),
+        ],
+    )
+    pieces = exchange(packed)
+
+    rows_out = pair + EXTRA
+    out_shape = [
         shape_of((heads, tokens_dev, width), BF),
-        (z, head, queries, keys, values, cotangent),
-        [SM] * 2 + [ANY] * 4,
-        "pack",
-        [pltpu.VMEM((4, tokens_dev, features), BF), pltpu.SemaphoreType.DMA((4,))],
-    )
-    x = lax.all_to_all(packed, HEAD, 0, 0, tiled=True).reshape(count, width)
-
-    rows_out = pair + EXTRA
-    out_shape = [shape_of((rows_out, marks), BF)]
+        shape_of((count, marks), BF),
+        shape_of((rows_out, marks), BF),
+    ]
     if ring:
         out_shape += [shape_of((rows_out, marks + pair), BF)] * 2
-    out_shape.append(shape_of((count, marks), BF))
-    mid, *halo_outs, expo = call(
-        local_sums_kernel, out_shape, (head, x, w_proj), [SM, VM, VM], "local_sums"
-    )
+    x, expo, mid, *halo_outs = call(
+        functools.partial(local_sums_kernel, heads=heads),
+        out_shape,
+        (head, w_head, *pieces),
+        [SM] + [VM] * (heads + 1),
+        "local_sums",
+    )
+    x = x.reshape(count, width)
 
     def shifted(block, shift):
         return lax.ppermute(block, SEQ, [(i, (i + shift) % seqs) for i in range(seqs)])
@@ -529,7 +578,7 @@
             shape_of((pair, 2 * count), BF),
             shape_of((2 * pair, pair), F32),
         ],
-        (x, ln_gain, ln_bias),
+        (x, gain, bias),
         [VM] * 3,
         "window_forward",
         flops=3 * work,
@@ -564,35 +613,43 @@
         flops=5 * work,
     )
     send_rows = tokens_dev + 8 + (dh // 4 if tiled else 0)
-    out_shape = [shape_of((heads, send_rows, width), BF)]
+    out_shape = [shape_of((send_rows, width), BF)] * heads
     if not tiled:
         out_shape.append(shape_of((dh, marks), F32))
-    send, *proj = call(
+    sent = call(
         functools.partial(
             final_kernel,
             ring=ring,
             seqs=seqs,
+            heads=heads,
             sub=sub if tiled else 1,
             parts=parts,
             tiled=tiled,
         ),
         out_shape,
-        (z, head, *grads, x, w_proj, affine, expo, od, dkvt, stats),
+        (z, head, *grads, x, w_head, affine, expo, od, dkvt, stats),
         [SM, SM] + [VM] * (len(grads) + 7),
         "landmark_backward",
-        [pltpu.VMEM((seqs, pair, marks), BF)] if ring else [],
-    )
-    back = lax.all_to_all(send, HEAD, 0, 0, tiled=True)
+        [pltpu.VMEM((heads, send_rows, width), BF)]
+        + ([pltpu.VMEM((seqs, pair, marks), BF)] if ring else []),
+    )
+    back = exchange(sent[:heads])
     out_shape = [shape_of((tokens_dev, features), BF)] * 4 + [shape_of((4, dh), F32)]
     if tiled:
         out_shape.append(shape_of((1, heads, dh, wide_part), F32))
     attended, dq, dk, dv, grad_norm, *tiles = call(
-        unpack_kernel, out_shape, (back,), [VM], "unpack", keep=False
+        functools.partial(unpack_kernel, heads=heads),
+        out_shape,
+        (head, *back),
+        [SM] + [VM] * heads,
+        "unpack",
+        [pltpu.VMEM((heads, send_rows, width), BF)],
+        keep=False,
     )
     if tiled:
         grad_proj = tiles[0]
     else:
-        full = lax.all_gather(proj[0], HEAD)
+        full = lax.all_gather(sent[-1], HEAD)
         inner = ("half", "part") if halves > 1 else "part"
         grad_proj = lax.psum_scatter(full, inner, scatter_dimension=2, tiled=True)[None] / parts
     return (attended, dq, dk, dv, grad_proj, grad_norm)

time: 56 us -> 53.7 us (0.959)
  blocking collectives: 27.2 us -> 0 us
  starting transfers between devices: 8.54 us -> 22.3 us
  waiting for transfers between devices: 8.69 us -> 19.9 us
    all_to_all x2 -> x0, blocking collectives: 27.2 us -> none  [the longest x1 14 us: per_device(): x = lax.all_to_all(packed, HEAD, 0, 0, tiled=True).reshape(count, width)]
    ppermute x0 -> x14, starting transfers between devices: none -> 13.7 us  [exchange(): out[k] = lax.ppermute(pieces[k], HEAD, [(i, i ^ k) for i in range(heads)])]
    ppermute x0 -> x14, waiting for transfers between devices: none -> 10.5 us  [exchange(): out[k] = lax.ppermute(pieces[k], HEAD, [(i, i ^ k) for i in range(heads)])]
    ppermute x6, waiting for transfers between devices: 8.69 us -> 9.37 us  [shifted(): lax.ppermute(block, SEQ, [(i, (i + shift) % seqs) for i in range(seqs)])]
  transfers between devices with their start and end apart: 6 -> 20, of which waited for: 2 -> 10; matrix products, arithmetic and copies ran while one was open for 0% -> 0% of each run, Pallas kernels for 8% -> 8%
where the time goes in v4:
time: 53.7 us; the launch traced here: 53.6 us
  starting transfers between devices  22.3 us (42%)
  waiting for transfers between devices  19.9 us (37%)
  Pallas kernels  10.8 us (20%)
  between operations  0.72 us (1%)
    ppermute x14, starting transfers between devices, exchange(): out[k] = lax.ppermute(pieces[k], HEAD, [(i, i ^ k) for i in range(heads)])  13.7 us
    pallas_call x7, Pallas kernels, call(): pl.pallas_call(kernel, out_shape=out_shape, in_specs=specs, out_specs=jax...  10.8 us
    ppermute x14, waiting for transfers between devices, exchange(): out[k] = lax.ppermute(pieces[k], HEAD, [(i, i ^ k) for i in range(heads)])  10.5 us
    ppermute x6, waiting for transfers between devices, shifted(): lax.ppermute(block, SEQ, [(i, (i + shift) % seqs) for i in range(seqs)])  9.37 us
    ppermute x6, starting transfers between devices, shifted(): lax.ppermute(block, SEQ, [(i, (i + shift) % seqs) for i in range(seqs)])  8.54 us
  transfers between devices with their start and end apart: 20, of which 10 were waited for; matrix products, arithmetic and copies ran while one was open for 0% of the time, Pallas kernels for 8%

profile of v4, /device:TPU:0, one launch (start us, length us, event | category | flops | bytes accessed | tf_op | source)
XLA Modules:
  0.0 53.6 jit_solution(3968079978064426477)
XLA Ops:
  0.6 1.6 %pack.1 = (bf16[128,256]{1,0:T(8,128)(2,1)S(1)}, bf16[128,256]{1,0:T(8,128)(2,1)S(1)}, bf16[128,256]{1,0:T(8,128)(2,1)S(1)}, bf16[128,256]{1,0:T(8,128)(2,1)S(1)...) custom-call(s32[1]{0:T(128)} %bitcast.head_ref.refs_1_, ...), custom_call_target="tpu_custom_call" | custom-call | tf_op jit(solution)/shard_map/pack/pallas_call | solution.py:485
  2.8 2.6 %collective-permute-start.1 = (bf16[128,256]{1,0:T(8,128)(2,1)S(1)}, bf16[128,256]{1,0:T(8,128)(2,1)S(1)}, u32[]{:S(2)}, u32[]{:S(2)}) collective-permute-start(bf16[128,256]{1,0:T(8,128)(2,1)S(1)} %get-tuple-element.51), channel_id=1, source_target_pairs={{0,2},{1,3},{2,0},{3,1},{4,6},{5,7},{6,4},{7,5},{8,10},{9,11},{10,... | collective-permute-start | bytes 196616 | tf_op jit(solution)/shard_map/ppermute | solution.py:519
  5.4 1.7 %collective-permute-start.3 = (bf16[128,256]{1,0:T(8,128)(2,1)S(1)}, bf16[128,256]{1,0:T(8,128)(2,1)S(1)}, u32[]{:S(2)}, u32[]{:S(2)}) collective-permute-start(bf16[128,256]{1,0:T(8,128)(2,1)S(1)} %get-tuple-element.53), channel_id=1, source_target_pairs={{0,4},{1,5},{2,6},{3,7},{4,0},{5,1},{6,2},{7,3},{8,12},{9,13},{10,... | collective-permute-start | bytes 196616 | tf_op jit(solution)/shard_map/ppermute | solution.py:519
  7.1 2.7 %collective-permute-start.5 = (bf16[128,256]{1,0:T(8,128)(2,1)S(1)}, bf16[128,256]{1,0:T(8,128)(2,1)S(1)}, u32[]{:S(2)}, u32[]{:S(2)}) collective-permute-start(bf16[128,256]{1,0:T(8,128)(2,1)S(1)} %get-tuple-element.55), channel_id=1, source_target_pairs={{0,6},{1,7},{2,4},{3,5},{4,2},{5,3},{6,0},{7,1},{8,14},{9,15},{10,... | collective-permute-start | bytes 196616 | tf_op jit(solution)/shard_map/ppermute | solution.py:519
  9.9 1.3 %collective-permute-done.4.refs_5_ = bf16[128,256]{1,0:T(8,128)(2,1)S(1)} collective-permute-done((bf16[128,256]{1,0:T(8,128)(2,1)S(1)}, bf16[128,256]{1,0:T(8,128)(2,1)S(1)}, u32[]{:S(2)}, u32[]{:S(2)}) %collective-permute-start.4) | collective-permute-done | bytes 65568 | tf_op jit(solution)/shard_map/ppermute | solution.py:519
  11.2 2.8 %collective-permute-done.5.refs_6_ = bf16[128,256]{1,0:T(8,128)(2,1)S(1)} collective-permute-done((bf16[128,256]{1,0:T(8,128)(2,1)S(1)}, bf16[128,256]{1,0:T(8,128)(2,1)S(1)}, u32[]{:S(2)}, u32[]{:S(2)}) %collective-permute-start.5) | collective-permute-done | bytes 65568 | tf_op jit(solution)/shard_map/ppermute | solution.py:519
  14.0 1.0 %collective-permute-done.6.refs_7_ = bf16[128,256]{1,0:T(8,128)(2,1)S(1)} collective-permute-done((bf16[128,256]{1,0:T(8,128)(2,1)S(1)}, bf16[128,256]{1,0:T(8,128)(2,1)S(1)}, u32[]{:S(2)}, u32[]{:S(2)}) %collective-permute-start.6) | collective-permute-done | bytes 65568 | tf_op jit(solution)/shard_map/ppermute | solution.py:519
  15.9 1.6 %collective-permute-start.7 = (bf16[136,384]{1,0:T(8,128)(2,1)S(1)}, bf16[136,384]{1,0:T(8,128)(2,1)S(1)}, u32[]{:S(2)}, u32[]{:S(2)}) collective-permute-start(bf16[136,384]{1,0:T(8,128)(2,1)S(1)} %get-tuple-element.64), channel_id=1, source_target_pairs={{0,8},{8,16},{16,24},{24,0},{1,9},{9,17},{17,25},{25,1},{2,10},{10... | collective-permute-start | bytes 313352 | tf_op jit(solution)/shard_map/ppermute | solution.py:556
  17.5 2.2 %collective-permute-start.9 = (bf16[136,384]{1,0:T(8,128)(2,1)S(1)}, bf16[136,384]{1,0:T(8,128)(2,1)S(1)}, u32[]{:S(2)}, u32[]{:S(2)}) collective-permute-start(bf16[136,384]{1,0:T(8,128)(2,1)S(1)} %get-tuple-element.65), channel_id=1, source_target_pairs={{0,24},{8,0},{16,8},{24,16},{1,25},{9,1},{17,9},{25,17},{2,26},{10... | collective-permute-start | bytes 313352 | tf_op jit(solution)/shard_map/ppermute | solution.py:556
  20.6 2.2 %window_forward.1 = (f32[1024,512]{1,0:T(8,128)S(1)}, bf16[2048,128]{1,0:T(8,128)(2,1)S(1)}, bf16[128,2048]{1,0:T(8,128)(2,1)S(1)}, f32[256,128]{1,0:T(8,128)S(1)}) custom-call(bf16[1024,256]{1,0:T(8,128)(2,1)S(1)} %bitcast.3, f32[2,64]{1,0:T(2,128)S(1)} %get-tuple-element.58.gain_src, f32[2,64]{1,0:T(2,128)S(1)} %get-tuple-element.59.bias_src), custom_call_target="tpu_custom_call" | custom-call | flops 301989888 | tf_op jit(solution)/shard_map/window_forward/pallas_call | solution.py:485
  22.8 5.2 %collective-permute-done.8.refs_6_ = bf16[136,256]{1,0:T(8,128)(2,1)S(1)} collective-permute-done((bf16[136,256]{1,0:T(8,128)(2,1)S(1)}, bf16[136,256]{1,0:T(8,128)(2,1)S(1)}, u32[]{:S(2)}, u32[]{:S(2)}) %collective-permute-start.8) | collective-permute-done | bytes 69664 | tf_op jit(solution)/shard_map/ppermute | solution.py:556
  28.0 1.9 %landmark_forward.1 = (f32[1024,128]{1,0:T(8,128)S(1)}, f32[1024,256]{1,0:T(8,128)S(1)}, bf16[128,256]{1,0:T(8,128)(2,1)S(1)}, bf16[128,384]{1,0:T(8,128)(2,1)S(...) custom-call(s32[1]{0:T(128)} %bitcast.1.z_ref.refs_0_, f32[1024,512]{1,0:T(8,128)S(1)} %get-tuple-element.60.refs_1_, ...), custom_call_target="tpu_custom_call" | custom-call | tf_op jit(solution)/shard_map/landmark_forward/pallas_call | solution.py:485
  30.0 3.8 %collective-permute-start.12 = (bf16[128,384]{1,0:T(8,128)(2,1)S(1)}, bf16[128,384]{1,0:T(8,128)(2,1)S(1)}, u32[]{:S(2)}, u32[]{:S(2)}) collective-permute-start(bf16[128,384]{1,0:T(8,128)(2,1)S(1)} %get-tuple-element.69), channel_id=1, source_target_pairs={{0,24},{8,0},{16,8},{24,16},{1,25},{9,1},{17,9},{25,17},{2,26},{10... | collective-permute-start | bytes 294920 | tf_op jit(solution)/shard_map/ppermute | solution.py:556
  33.8 2.1 %window_backward.1 = (bf16[1024,128]{1,0:T(8,128)(2,1)S(1)}, f32[128,1024]{1,0:T(8,128)S(1)}) custom-call(bf16[1024,256]{1,0:T(8,128)(2,1)S(1)} %bitcast.4, bf16[2048,128]{1,0:T(8,128)(2,1)S(1)} %get-tuple-element.61.refs_2_.a_ref, bf16[128,2048]{1,0:T(8,128)(2,1)S(1)} %get-tuple-element.62.refs_3_.at_ref, f32[1024,128]{1,0:T(8,128)S(1)} %get-tuple-element.71.late_ref, ...), custom_call_target="tpu_custom_call" | custom-call | flops 503316480 | tf_op jit(solution)/shard_map/window_backward/pallas_call | solution.py:485
  35.9 4.2 %collective-permute-done.11.refs_4_ = bf16[128,256]{1,0:T(8,128)(2,1)S(1)} collective-permute-done((bf16[128,256]{1,0:T(8,128)(2,1)S(1)}, bf16[128,256]{1,0:T(8,128)(2,1)S(1)}, u32[]{:S(2)}, u32[]{:S(2)}) %collective-permute-start.11) | collective-permute-done | bytes 65568 | tf_op jit(solution)/shard_map/ppermute | solution.py:556
  40.1 0.9 %landmark_backward.1 = (bf16[152,256]{1,0:T(8,128)(2,1)S(1)}, bf16[152,256]{1,0:T(8,128)(2,1)S(1)}, bf16[152,256]{1,0:T(8,128)(2,1)S(1)}, bf16[152,256]{1,0:T(8,...) custom-call(s32[1]{0:T(128)} %bitcast.1.z_ref.refs_0_, ...), custom_call_target="tpu_custom_call" | custom-call | tf_op jit(solution)/shard_map/landmark_backward/pallas_call | solution.py:485
  41.7 1.2 %collective-permute-start.15 = (bf16[152,256]{1,0:T(8,128)(2,1)S(1)}, bf16[152,256]{1,0:T(8,128)(2,1)S(1)}, u32[]{:S(2)}, u32[]{:S(2)}) collective-permute-start(bf16[152,256]{1,0:T(8,128)(2,1)S(1)} %get-tuple-element.79), channel_id=1, source_target_pairs={{0,3},{1,2},{2,1},{3,0},{4,7},{5,6},{6,5},{7,4},{8,11},{9,10},{10,... | collective-permute-start | bytes 233480 | tf_op jit(solution)/shard_map/ppermute | solution.py:519
  42.9 1.3 %collective-permute-start.16 = (bf16[152,256]{1,0:T(8,128)(2,1)S(1)}, bf16[152,256]{1,0:T(8,128)(2,1)S(1)}, u32[]{:S(2)}, u32[]{:S(2)}) collective-permute-start(bf16[152,256]{1,0:T(8,128)(2,1)S(1)} %get-tuple-element.80), channel_id=1, source_target_pairs={{0,4},{1,5},{2,6},{3,7},{4,0},{5,1},{6,2},{7,3},{8,12},{9,13},{10,... | collective-permute-start | bytes 233480 | tf_op jit(solution)/shard_map/ppermute | solution.py:519
  44.6 1.5 %collective-permute-start.18 = (bf16[152,256]{1,0:T(8,128)(2,1)S(1)}, bf16[152,256]{1,0:T(8,128)(2,1)S(1)}, u32[]{:S(2)}, u32[]{:S(2)}) collective-permute-start(bf16[152,256]{1,0:T(8,128)(2,1)S(1)} %get-tuple-element.82), channel_id=1, source_target_pairs={{0,6},{1,7},{2,4},{3,5},{4,2},{5,3},{6,0},{7,1},{8,14},{9,15},{10,... | collective-permute-start | bytes 233480 | tf_op jit(solution)/shard_map/ppermute | solution.py:519
  46.4 1.0 %collective-permute-start.19 = (bf16[152,256]{1,0:T(8,128)(2,1)S(1)}, bf16[152,256]{1,0:T(8,128)(2,1)S(1)}, u32[]{:S(2)}, u32[]{:S(2)}) collective-permute-start(bf16[152,256]{1,0:T(8,128)(2,1)S(1)} %get-tuple-element.83), channel_id=1, source_target_pairs={{0,7},{1,6},{2,5},{3,4},{4,3},{5,2},{6,1},{7,0},{8,15},{9,14},{10,... | collective-permute-start | bytes 233480 | tf_op jit(solution)/shard_map/ppermute | solution.py:519
  47.9 1.0 %collective-permute-done.17.refs_5_ = bf16[152,256]{1,0:T(8,128)(2,1)S(1)} collective-permute-done((bf16[152,256]{1,0:T(8,128)(2,1)S(1)}, bf16[152,256]{1,0:T(8,128)(2,1)S(1)}, u32[]{:S(2)}, u32[]{:S(2)}) %collective-permute-start.17) | collective-permute-done | bytes 77856 | tf_op jit(solution)/shard_map/ppermute | solution.py:519
  48.9 2.1 %collective-permute-done.18.refs_6_ = bf16[152,256]{1,0:T(8,128)(2,1)S(1)} collective-permute-done((bf16[152,256]{1,0:T(8,128)(2,1)S(1)}, bf16[152,256]{1,0:T(8,128)(2,1)S(1)}, u32[]{:S(2)}, u32[]{:S(2)}) %collective-permute-start.18) | collective-permute-done | bytes 77856 | tf_op jit(solution)/shard_map/ppermute | solution.py:519
  51.0 1.4 %collective-permute-done.19.refs_7_ = bf16[152,256]{1,0:T(8,128)(2,1)S(1)} collective-permute-done((bf16[152,256]{1,0:T(8,128)(2,1)S(1)}, bf16[152,256]{1,0:T(8,128)(2,1)S(1)}, u32[]{:S(2)}, u32[]{:S(2)}) %collective-permute-start.19) | collective-permute-done | bytes 77856 | tf_op jit(solution)/shard_map/ppermute | solution.py:519
  52.4 1.2 %unpack.1 = (bf16[128,512]{1,0:T(8,128)(2,1)}, bf16[128,512]{1,0:T(8,128)(2,1)}, bf16[128,512]{1,0:T(8,128)(2,1)}, bf16[128,512]{1,0:T(8,128)(2,1)}, f32[4,64]{1,0:T(4,128)}, /*index=5*/f32[1,8,64,64]{3,2,1,0:T(8,128)}) custom-call(s32[1]{0:T(128)} %bitcast.head_ref.refs_1_, bf16[152,256]{1,0:T(8,128)(2,1)S(1)} %get-tuple-element.76.refs_0_, ...), custom_call_target="tpu_custom_call" | custom-call | tf_op jit(solution)/shard_map/unpack/pallas_call | solution.py:485
  (23 shorter events, 4.3 us)
Async XLA Ops:
  2.2 4.9 %collective-permute-start = (bf16[128,256]{1,0:T(8,128)(2,1)S(1)}, bf16[128,256]{1,0:T(8,128)(2,1)S(1)}, u32[]{:S(2)}, u32[]{:S(2)}) collective-permute-start(bf16[128,256]{1,0:T(8,128)(2,1)S(1)} %get-tuple-element.50), channel_id=1, source_target_pairs={{0,1},{1,0},{2,3},{3,2},{4,5},{5,4},{6,7},{7,6},{8,9},{9,8},{10,11... | collective-permute-start | bytes 196616 | tf_op jit(solution)/shard_map/ppermute | solution.py:519
  2.8 7.0 %collective-permute-start.1 = (bf16[128,256]{1,0:T(8,128)(2,1)S(1)}, bf16[128,256]{1,0:T(8,128)(2,1)S(1)}, u32[]{:S(2)}, u32[]{:S(2)}) collective-permute-start(bf16[128,256]{1,0:T(8,128)(2,1)S(1)} %get-tuple-element.51), channel_id=1, source_target_pairs={{0,2},{1,3},{2,0},{3,1},{4,6},{5,7},{6,4},{7,5},{8,10},{9,11},{10,... | collective-permute-start | bytes 196616 | tf_op jit(solution)/shard_map/ppermute | solution.py:519
  5.3 4.5 %collective-permute-start.2 = (bf16[128,256]{1,0:T(8,128)(2,1)S(1)}, bf16[128,256]{1,0:T(8,128)(2,1)S(1)}, u32[]{:S(2)}, u32[]{:S(2)}) collective-permute-start(bf16[128,256]{1,0:T(8,128)(2,1)S(1)} %get-tuple-element.52), channel_id=1, source_target_pairs={{0,3},{1,2},{2,1},{3,0},{4,7},{5,6},{6,5},{7,4},{8,11},{9,10},{10,... | collective-permute-start | bytes 196616 | tf_op jit(solution)/shard_map/ppermute | solution.py:519
  5.4 4.5 %collective-permute-start.3 = (bf16[128,256]{1,0:T(8,128)(2,1)S(1)}, bf16[128,256]{1,0:T(8,128)(2,1)S(1)}, u32[]{:S(2)}, u32[]{:S(2)}) collective-permute-start(bf16[128,256]{1,0:T(8,128)(2,1)S(1)} %get-tuple-element.53), channel_id=1, source_target_pairs={{0,4},{1,5},{2,6},{3,7},{4,0},{5,1},{6,2},{7,3},{8,12},{9,13},{10,... | collective-permute-start | bytes 196616 | tf_op jit(solution)/shard_map/ppermute | solution.py:519
  7.1 4.1 %collective-permute-start.4 = (bf16[128,256]{1,0:T(8,128)(2,1)S(1)}, bf16[128,256]{1,0:T(8,128)(2,1)S(1)}, u32[]{:S(2)}, u32[]{:S(2)}) collective-permute-start(bf16[128,256]{1,0:T(8,128)(2,1)S(1)} %get-tuple-element.54), channel_id=1, source_target_pairs={{0,5},{1,4},{2,7},{3,6},{4,1},{5,0},{6,3},{7,2},{8,13},{9,12},{10,... | collective-permute-start | bytes 196616 | tf_op jit(solution)/shard_map/ppermute | solution.py:519
  7.1 6.9 %collective-permute-start.5 = (bf16[128,256]{1,0:T(8,128)(2,1)S(1)}, bf16[128,256]{1,0:T(8,128)(2,1)S(1)}, u32[]{:S(2)}, u32[]{:S(2)}) collective-permute-start(bf16[128,256]{1,0:T(8,128)(2,1)S(1)} %get-tuple-element.55), channel_id=1, source_target_pairs={{0,6},{1,7},{2,4},{3,5},{4,2},{5,3},{6,0},{7,1},{8,14},{9,15},{10,... | collective-permute-start | bytes 196616 | tf_op jit(solution)/shard_map/ppermute | solution.py:519
  9.8 5.3 %collective-permute-start.6 = (bf16[128,256]{1,0:T(8,128)(2,1)S(1)}, bf16[128,256]{1,0:T(8,128)(2,1)S(1)}, u32[]{:S(2)}, u32[]{:S(2)}) collective-permute-start(bf16[128,256]{1,0:T(8,128)(2,1)S(1)} %get-tuple-element.56), channel_id=1, source_target_pairs={{0,7},{1,6},{2,5},{3,4},{4,3},{5,2},{6,1},{7,0},{8,15},{9,14},{10,... | collective-permute-start | bytes 196616 | tf_op jit(solution)/shard_map/ppermute | solution.py:519
  15.9 12.1 %collective-permute-start.7 = (bf16[136,384]{1,0:T(8,128)(2,1)S(1)}, bf16[136,384]{1,0:T(8,128)(2,1)S(1)}, u32[]{:S(2)}, u32[]{:S(2)}) collective-permute-start(bf16[136,384]{1,0:T(8,128)(2,1)S(1)} %get-tuple-element.64), channel_id=1, source_target_pairs={{0,8},{8,16},{16,24},{24,0},{1,9},{9,17},{17,25},{25,1},{2,10},{10... | collective-permute-start | bytes 313352 | tf_op jit(solution)/shard_map/ppermute | solution.py:556
  17.5 10.5 %collective-permute-start.9 = (bf16[136,384]{1,0:T(8,128)(2,1)S(1)}, bf16[136,384]{1,0:T(8,128)(2,1)S(1)}, u32[]{:S(2)}, u32[]{:S(2)}) collective-permute-start(bf16[136,384]{1,0:T(8,128)(2,1)S(1)} %get-tuple-element.65), channel_id=1, source_target_pairs={{0,24},{8,0},{16,8},{24,16},{1,25},{9,1},{17,9},{25,17},{2,26},{10... | collective-permute-start | bytes 313352 | tf_op jit(solution)/shard_map/ppermute | solution.py:556
  19.8 8.2 %collective-permute-start.8 = (bf16[136,256]{1,0:T(8,128)(2,1)S(1)}, bf16[136,256]{1,0:T(8,128)(2,1)S(1)}, u32[]{:S(2)}, u32[]{:S(2)}) collective-permute-start(bf16[136,256]{1,0:T(8,128)(2,1)S(1)} %get-tuple-element.63.refs_4_), channel_id=1, source_target_pairs={{0,16},{8,24},{16,0},{24,8},{1,17},{9,25},{17,1},{25,9},{2,18},{10... | collective-permute-start | bytes 208904 | tf_op jit(solution)/shard_map/ppermute | solution.py:556
  29.9 10.2 %collective-permute-start.10 = (bf16[128,384]{1,0:T(8,128)(2,1)S(1)}, bf16[128,384]{1,0:T(8,128)(2,1)S(1)}, u32[]{:S(2)}, u32[]{:S(2)}) collective-permute-start(bf16[128,384]{1,0:T(8,128)(2,1)S(1)} %get-tuple-element.68), channel_id=1, source_target_pairs={{0,8},{8,16},{16,24},{24,0},{1,9},{9,17},{17,25},{25,1},{2,10},{10... | collective-permute-start | bytes 294920 | tf_op jit(solution)/shard_map/ppermute | solution.py:556
  30.0 10.1 %collective-permute-start.12 = (bf16[128,384]{1,0:T(8,128)(2,1)S(1)}, bf16[128,384]{1,0:T(8,128)(2,1)S(1)}, u32[]{:S(2)}, u32[]{:S(2)}) collective-permute-start(bf16[128,384]{1,0:T(8,128)(2,1)S(1)} %get-tuple-element.69), channel_id=1, source_target_pairs={{0,24},{8,0},{16,8},{24,16},{1,25},{9,1},{17,9},{25,17},{2,26},{10... | collective-permute-start | bytes 294920 | tf_op jit(solution)/shard_map/ppermute | solution.py:556
  33.8 6.3 %collective-permute-start.11 = (bf16[128,256]{1,0:T(8,128)(2,1)S(1)}, bf16[128,256]{1,0:T(8,128)(2,1)S(1)}, u32[]{:S(2)}, u32[]{:S(2)}) collective-permute-start(bf16[128,256]{1,0:T(8,128)(2,1)S(1)} %get-tuple-element.67.refs_2_), channel_id=1, source_target_pairs={{0,16},{8,24},{16,0},{24,8},{1,17},{9,25},{17,1},{25,9},{2,18},{10... | collective-permute-start | bytes 196616 | tf_op jit(solution)/shard_map/ppermute | solution.py:556
  41.0 3.6 %collective-permute-start.13 = (bf16[152,256]{1,0:T(8,128)(2,1)S(1)}, bf16[152,256]{1,0:T(8,128)(2,1)S(1)}, u32[]{:S(2)}, u32[]{:S(2)}) collective-permute-start(bf16[152,256]{1,0:T(8,128)(2,1)S(1)} %get-tuple-element.77), channel_id=1, source_target_pairs={{0,1},{1,0},{2,3},{3,2},{4,5},{5,4},{6,7},{7,6},{8,9},{9,8},{10,11... | collective-permute-start | bytes 233480 | tf_op jit(solution)/shard_map/ppermute | solution.py:519
  41.1 5.3 %collective-permute-start.14 = (bf16[152,256]{1,0:T(8,128)(2,1)S(1)}, bf16[152,256]{1,0:T(8,128)(2,1)S(1)}, u32[]{:S(2)}, u32[]{:S(2)}) collective-permute-start(bf16[152,256]{1,0:T(8,128)(2,1)S(1)} %get-tuple-element.78), channel_id=1, source_target_pairs={{0,2},{1,3},{2,0},{3,1},{4,6},{5,7},{6,4},{7,5},{8,10},{9,11},{10,... | collective-permute-start | bytes 233480 | tf_op jit(solution)/shard_map/ppermute | solution.py:519
  41.7 5.7 %collective-permute-start.15 = (bf16[152,256]{1,0:T(8,128)(2,1)S(1)}, bf16[152,256]{1,0:T(8,128)(2,1)S(1)}, u32[]{:S(2)}, u32[]{:S(2)}) collective-permute-start(bf16[152,256]{1,0:T(8,128)(2,1)S(1)} %get-tuple-element.79), channel_id=1, source_target_pairs={{0,3},{1,2},{2,1},{3,0},{4,7},{5,6},{6,5},{7,4},{8,11},{9,10},{10,... | collective-permute-start | bytes 233480 | tf_op jit(solution)/shard_map/ppermute | solution.py:519
  42.9 5.0 %collective-permute-start.16 = (bf16[152,256]{1,0:T(8,128)(2,1)S(1)}, bf16[152,256]{1,0:T(8,128)(2,1)S(1)}, u32[]{:S(2)}, u32[]{:S(2)}) collective-permute-start(bf16[152,256]{1,0:T(8,128)(2,1)S(1)} %get-tuple-element.80), channel_id=1, source_target_pairs={{0,4},{1,5},{2,6},{3,7},{4,0},{5,1},{6,2},{7,3},{8,12},{9,13},{10,... | collective-permute-start | bytes 233480 | tf_op jit(solution)/shard_map/ppermute | solution.py:519
  44.2 4.7 %collective-permute-start.17 = (bf16[152,256]{1,0:T(8,128)(2,1)S(1)}, bf16[152,256]{1,0:T(8,128)(2,1)S(1)}, u32[]{:S(2)}, u32[]{:S(2)}) collective-permute-start(bf16[152,256]{1,0:T(8,128)(2,1)S(1)} %get-tuple-element.81), channel_id=1, source_target_pairs={{0,5},{1,4},{2,7},{3,6},{4,1},{5,0},{6,3},{7,2},{8,13},{9,12},{10,... | collective-permute-start | bytes 233480 | tf_op jit(solution)/shard_map/ppermute | solution.py:519
  44.6 6.3 %collective-permute-start.18 = (bf16[152,256]{1,0:T(8,128)(2,1)S(1)}, bf16[152,256]{1,0:T(8,128)(2,1)S(1)}, u32[]{:S(2)}, u32[]{:S(2)}) collective-permute-start(bf16[152,256]{1,0:T(8,128)(2,1)S(1)} %get-tuple-element.82), channel_id=1, source_target_pairs={{0,6},{1,7},{2,4},{3,5},{4,2},{5,3},{6,0},{7,1},{8,14},{9,15},{10,... | collective-permute-start | bytes 233480 | tf_op jit(solution)/shard_map/ppermute | solution.py:519
  46.4 6.0 %collective-permute-start.19 = (bf16[152,256]{1,0:T(8,128)(2,1)S(1)}, bf16[152,256]{1,0:T(8,128)(2,1)S(1)}, u32[]{:S(2)}, u32[]{:S(2)}) collective-permute-start(bf16[152,256]{1,0:T(8,128)(2,1)S(1)} %get-tuple-element.83), channel_id=1, source_target_pairs={{0,7},{1,6},{2,5},{3,4},{4,3},{5,2},{6,1},{7,0},{8,15},{9,14},{10,... | collective-permute-start | bytes 233480 | tf_op jit(solution)/shard_map/ppermute | solution.py:519
